TPU v7x, 32 devices: a whole 2x2x4 slice. The times are simulated.
32 devices in a mesh: spec: 4 (over y, core), lat: 8 (over z, x).
Axes of the slice: x: 2, y: 2, z: 4, core: 2. Of those that a mesh axis runs over, the one named last changes fastest.
Arguments:
- concentration: float32 [256, 32, 512], P('spec', 'lat'), may hold values from 0.05 to 2
- courant: float32 [32, 512], P('lat'), may hold values from -0.9 to 0.9
- rate_const: float32 [1024], replicated, may hold values from 0.005 to 0.08
- reactants: int32 [1024, 2], replicated, may hold values from 0 to 255
- products: int32 [1024, 2], replicated, may hold values from 0 to 255
- daylit: int32 [32], replicated, may hold values from 0 to 1, as said below
- block_slot: int32 [32], replicated, may hold values from 0 to 31, as said below
Outputs:
- states: float32 [256, 32, 512], P(None, 'lat', 'spec')
Inputs may be any that keep to these rules, and one draw needn't show every extreme that they name: block_slot is a permutation of the 32 rows. Grouping rows into groups of 4 in order, every row's slot lies in its own group or in the group just before or after it, and every group moves exactly one row into each neighbouring group that exists. Of the 4 slots of every group, exactly 2 are taken by rows with daylit equal to 1.
All inputs are finite; a program needn't handle non-finite values.
Results may differ from a plain program's by a relative error of at most 0.0003.
Values sent between devices are 32-bit elements; how exact they have to be, the bound alone decides.
No kernel may reach another device: no remote copies, remote signals or barrier semaphores. Data moves between devices by JAX's collectives and lax.ppermute only.
A program may use at most 64 MiB of HBM per device.

v0:
```python
import functools

import jax
import jax.numpy as jnp
from jax import lax
from jax.experimental import pallas as pl
from jax.experimental.pallas import tpu as pltpu
from jax.sharding import Mesh
from jax.sharding import PartitionSpec as P


SUBSTEPS = 2
PAIR = 2
LANES = 128
VMEM = pl.BlockSpec(memory_space=pltpu.VMEM)
SMEM = pl.BlockSpec(memory_space=pltpu.SMEM)


def params(mib):
    return pltpu.CompilerParams(vmem_limit_bytes=mib * 1024 * 1024)


def table_kernel(
    react_ref, prod_ref, const_ref, slot_ref, day_ref, take_ref, net_ref, rate_ref, plan_ref, source_of, lit_of
):
    note_plan(slot_ref, day_ref, plan_ref, source_of, lit_of)
    reactions, species = take_ref.shape[1:]
    width = rate_ref.shape[1]
    blocks, block = const_ref.shape
    const = jnp.transpose(const_ref[...])
    for at in range(blocks):
        rate_ref[at * block : (at + 1) * block, :] = jnp.broadcast_to(const[:, at : at + 1], (block, width))
    react = react_ref[...].astype(jnp.float32)
    prod = prod_ref[...].astype(jnp.float32)
    tall = lax.broadcasted_iota(jnp.int32, (8, reactions), 0)
    columns = jnp.transpose(jnp.where(tall == 0, react[0:1, :], react[1:2, :]))
    lane = lax.broadcasted_iota(jnp.int32, (reactions, species), 1).astype(jnp.float32)
    for side in range(2):
        hit = columns[:, side : side + 1] == lane
        take_ref[side] = jnp.where(hit, 1.0, 0.0).astype(take_ref.dtype)
    line = lax.broadcasted_iota(jnp.int32, (species, reactions), 0).astype(jnp.float32)

    def ones(row):
        return jnp.where(row == line, 1.0, 0.0)

    net = ones(prod[0:1, :]) + ones(prod[1:2, :]) - ones(react[0:1, :]) - ones(react[1:2, :])
    net_ref[...] = net.astype(net_ref.dtype)


def mechanism_tables(rate_const, reactants, products, block_slot, daylit, species, rows):
    reactions = reactants.shape[0]
    span = PAIR * rows
    return pl.pallas_call(
        table_kernel,
        out_shape=(
            jax.ShapeDtypeStruct((2, reactions, species), jnp.bfloat16),
            jax.ShapeDtypeStruct((species, reactions), jnp.bfloat16),
            jax.ShapeDtypeStruct((reactions, LANES), jnp.float32),
            jax.ShapeDtypeStruct((span + rows,), jnp.int32),
        ),
        in_specs=[VMEM, VMEM, VMEM, SMEM, SMEM],
        out_specs=(VMEM, VMEM, VMEM, SMEM),
        scratch_shapes=[pltpu.SMEM((span,), jnp.int32), pltpu.SMEM((span,), jnp.int32)],
        compiler_params=params(8),
        cost_estimate=pl.CostEstimate(flops=20_000_000, bytes_accessed=2_000_000, transcendentals=0),
        name="tables",
    )(reactants.T, products.T, rate_const.reshape(-1, LANES), block_slot, daylit)


def note_slots(slot_ref, day_ref, first_row, row_count, base_slot, source_of, lit_of):
    total = slot_ref.shape[0]
    slot_count = source_of.shape[0]
    for step in range(row_count):
        row = first_row + step
        held = jnp.clip(row, 0, total - 1)
        slot = slot_ref[held] - base_slot

        @pl.when((row >= 0) & (row < total) & (slot >= 0) & (slot < slot_count))
        def _():
            at = jnp.clip(slot, 0, slot_count - 1)
            source_of[at] = step
            lit_of[at] = day_ref[held]


def places(lit_of, first, rows):
    lit_seen = jnp.int32(0)
    dark_seen = jnp.int32(rows // 2)
    found = []
    for step in range(rows):
        lit = lit_of[first + step]
        found.append(jnp.clip(jnp.where(lit == 1, lit_seen, dark_seen), 0, rows - 1))
        lit_seen = lit_seen + lit
        dark_seen = dark_seen + 1 - lit
    return found


def note_plan(slot_ref, day_ref, plan_ref, source_of, lit_of):
    span = source_of.shape[0]
    rows = span // PAIR
    band = lax.axis_index("band")
    side = lax.axis_index("pair")
    reach = span // 2
    note_slots(slot_ref, day_ref, band * span - reach, span + 2 * reach, band * span, source_of, lit_of)
    for half in range(PAIR):
        for slot, place in enumerate(places(lit_of, half * rows, rows)):
            plan_ref[half * rows + place] = source_of[half * rows + slot]

            @pl.when(side == half)
            def _():
                plan_ref[span + place] = slot


def flat_rows(field):
    rows, columns = field.shape[-2:]
    field = field.reshape(-1, rows, columns // LANES, LANES)
    return field.transpose(0, 2, 1, 3).reshape(-1, LANES)


def pack_kernel(field_ref, flow_ref, own_ref, other_ref, sems):
    flow = flow_ref.shape[0]
    half = own_ref.shape[0] - flow
    side = lax.axis_index("pair")
    copies = []
    for at, (ref, which) in enumerate(((other_ref, 1 - side), (own_ref, side))):
        first = pl.multiple_of(which * half, 8)
        for to, source, count, sem in ((0, field_ref.at[pl.ds(first, half)], half, 2 * at), (half, flow_ref, flow, 2 * at + 1)):
            copies.append(pltpu.make_async_copy(source, ref.at[pl.ds(to, count)], sems.at[sem]))
    for copy in copies:
        copy.start()
    for copy in copies:
        copy.wait()


def pack(concentration, courant):
    field, flow = flat_rows(concentration), flat_rows(courant)
    field = pltpu.with_memory_space_constraint(field, pltpu.HBM)
    flow = pltpu.with_memory_space_constraint(flow, pltpu.HBM)
    out = jax.ShapeDtypeStruct((field.shape[0] // PAIR + flow.shape[0], LANES), jnp.float32)
    return pl.pallas_call(
        pack_kernel,
        out_shape=(out, out),
        in_specs=[pl.BlockSpec(memory_space=pltpu.HBM)] * 2,
        out_specs=(VMEM, VMEM),
        scratch_shapes=[pltpu.SemaphoreType.DMA((4,))],
        compiler_params=params(8),
        name="pack",
    )(field, flow)


def minmod(left, right):
    low = jnp.minimum(left, right)
    high = jnp.maximum(left, right)
    return jnp.maximum(low, 0.0) + jnp.minimum(high, 0.0)


def sweep(load, courant, store, first, count):
    older = load(first - 2)
    old = load(first - 1)
    step_old = old - older
    here = load(first)
    step_here = here - old
    slope_old = minmod(step_here, step_old)
    flux_old = None
    for row in range(first, first + count + 1):
        following = load(row + 1)
        step_next = following - here
        slope_here = minmod(step_next, step_here)
        number = courant(row)
        up = jnp.maximum(number, 0.0)
        down = jnp.minimum(number, 0.0)
        up_half = up * (0.5 * (1.0 - number))
        down_half = down * (-0.5 * (1.0 + number))
        flux = (up * old + up_half * slope_old) + (down * here + down_half * slope_here)
        if flux_old is not None:
            store(row - 1, old - (flux - flux_old))
        old, here, step_here, slope_old, flux_old = here, following, step_next, slope_here, flux


def advect_kernel(turn, held, own_ref, swap_ref, own_a, own_b, swap_a, swap_b, plan_ref, *refs):
    same_ref, cross_ref = refs[held : held + 2]
    window, flow, middle, advected, plan, sem = refs[2 * held + 2 :]
    fetch = pltpu.make_async_copy(plan_ref, plan, sem)
    fetch.start()
    rows, species, width = same_ref.shape
    span = PAIR * rows
    reach = span // 2
    band = lax.axis_index("band")
    side = lax.axis_index("pair")
    total = lax.axis_size("band") * span
    even = lax.rem(band, 2) == 0
    base_a = jnp.where(even, 2 * PAIR, 0)
    base_b = 2 * PAIR - base_a
    part = lax.bitwise_xor(lax.axis_index("spec"), turn)
    pieces = width // LANES
    apart = own_ref.shape[0] // (species + 1)
    for ref, place in (
        (own_ref, PAIR + side),
        (swap_ref, PAIR + 1 - side),
        (own_a, base_a + side),
        (own_b, base_b + side),
        (swap_a, base_a + 1 - side),
        (swap_b, base_b + 1 - side),
    ):
        for row in range(rows):
            for piece in range(pieces):
                at = (part * pieces + piece) * rows + row
                lanes = slice(piece * LANES, (piece + 1) * LANES)
                window[place * rows + row, :, lanes] = ref[pl.ds(at, species, stride=apart), :]
                flow[place * rows + row, :, lanes] = ref[pl.ds(species * apart + at, 1), :]

    first_row = band * span - span

    def courant(row):
        at = first_row + row
        return jnp.where((at >= 1) & (at <= total - 1), flow[row], 0.0)

    start = span - reach

    def store_middle(row, value):
        middle[row] = value

    def store_advected(row, value):
        advected[row - start] = value

    sweep(lambda row: window[row], courant, store_middle, start - 2, span + 2 * reach + 4)
    sweep(lambda row: middle[row], courant, store_advected, start, span + 2 * reach)
    fetch.wait()
    for place in range(rows):
        same_ref[place] = advected[plan[side * rows + place]]
        cross_ref[place] = advected[plan[(1 - side) * rows + place]]


def advect(turn, fields, plan, held, parts, rows, columns):
    species = fields[0].shape[0] * LANES // (rows * columns) - 1
    span = PAIR * rows
    width = columns // parts
    chunk = jax.ShapeDtypeStruct((rows, species, width), jnp.float32)
    return pl.pallas_call(
        functools.partial(advect_kernel, turn, len(held)),
        out_shape=(chunk, chunk) + (chunk,) * len(held),
        in_specs=[VMEM] * 7 + [pl.BlockSpec(memory_space=pl.ANY)] * len(held),
        out_specs=(VMEM, VMEM) + (pl.BlockSpec(memory_space=pl.ANY),) * len(held),
        input_output_aliases={7 + at: 2 + at for at in range(len(held))},
        scratch_shapes=[
            pltpu.VMEM((3 * span, species, width), jnp.float32),
            pltpu.VMEM((3 * span, 1, width), jnp.float32),
            pltpu.VMEM((3 * span, species, width), jnp.float32),
            pltpu.VMEM((2 * span, species, width), jnp.float32),
            pltpu.SMEM(plan.shape, jnp.int32),
            pltpu.SemaphoreType.DMA,
        ],
        compiler_params=params(8),
        cost_estimate=pl.CostEstimate(flops=4_000_000, bytes_accessed=400_000, transcendentals=0),
    )(*fields, plan, *held)


def split_rows(value):
    high = value.astype(jnp.bfloat16)
    low = (value - high.astype(jnp.float32)).astype(jnp.bfloat16)
    return jnp.concatenate([high, low], axis=0)


def twice(table):
    return jnp.concatenate([table, table], axis=1)


def dot(left, right):
    return jnp.dot(left, right, preferred_element_type=jnp.float32)


def chemistry_kernel(count, *refs):
    chunks = refs[:count]
    take_ref, net_ref, rate_ref, plan_ref, out_ref, cells, plan, sem = refs[count:]
    fetch = pltpu.make_async_copy(plan_ref, plan, sem)
    fetch.start()
    rows, lines, width = chunks[0].shape
    species = count * lines
    lit_rows = rows // 2
    copies = lit_rows * width // LANES
    spec = lax.axis_index("spec")
    side = lax.axis_index("pair")
    for at, chunk in enumerate(chunks):
        source = lax.bitwise_xor(spec, at // PAIR) * PAIR + lax.bitwise_xor(side, at % PAIR)
        first = pl.multiple_of(source * lines, lines)
        for place in range(lit_rows):
            cells[pl.ds(first, lines), place * width : (place + 1) * width] = chunk[place]

    conc = cells[...]
    const = jnp.concatenate([rate_ref[...]] * copies, axis=1)
    for _ in range(SUBSTEPS):
        parts = split_rows(conc)
        encounter = dot(twice(take_ref[0]), parts) * dot(twice(take_ref[1]), parts)
        rates = const * encounter / (1.0 + jnp.abs(encounter))
        conc = conc + dot(twice(net_ref[...]), split_rows(rates))
    fetch.wait()
    slot_of = [plan[PAIR * rows + place] for place in range(rows)]
    for at, chunk in enumerate(chunks):
        source = lax.bitwise_xor(spec, at // PAIR) * PAIR + lax.bitwise_xor(side, at % PAIR)
        for place in range(lit_rows, rows):
            out_ref[pl.ds(source * (lines * rows) + slot_of[place], lines, stride=rows), :] = chunk[place]
    for place in range(lit_rows):
        out_ref[pl.ds(slot_of[place], species, stride=rows), :] = conc[:, place * width : (place + 1) * width]


def chemistry(chunks, take, net, rates, plan):
    rows, lines, width = chunks[0].shape
    species = len(chunks) * lines
    flat = pl.pallas_call(
        functools.partial(chemistry_kernel, len(chunks)),
        out_shape=jax.ShapeDtypeStruct((species * rows, width), jnp.float32),
        in_specs=[VMEM] * (len(chunks) + 4),
        out_specs=VMEM,
        scratch_shapes=[
            pltpu.VMEM((species, rows // 2 * width), jnp.float32),
            pltpu.SMEM(plan.shape, jnp.int32),
            pltpu.SemaphoreType.DMA,
        ],
        compiler_params=params(16),
        name="chemistry",
    )(*chunks, take, net, rates, plan)
    return flat.reshape(species, rows, width)


def couples(count, first):
    pairs = []
    for low in range(first, count - 1, 2):
        pairs += [(low, low + 1), (low + 1, low)]
    return pairs


def on_device(concentration, courant, rate_const, reactants, products, daylit, block_slot):
    species_here, rows, columns = concentration.shape
    parts = lax.axis_size("spec")
    bands = lax.axis_size("band")
    own, other = pack(concentration, courant)
    swap = lax.ppermute(other, "pair", couples(PAIR, 0))
    own_a = lax.ppermute(own, "band", couples(bands, 0))
    own_b = lax.ppermute(own, "band", couples(bands, 1))
    swap_a = lax.ppermute(swap, "band", couples(bands, 0))
    swap_b = lax.ppermute(swap, "band", couples(bands, 1))
    take, net, rates, plan = mechanism_tables(
        rate_const, reactants, products, block_slot, daylit, species_here * parts, rows
    )
    fields = (own, swap, own_a, own_b, swap_a, swap_b)
    chunks = [None] * (parts * PAIR)

    def send(chunk, at):
        pairs = [(peer, peer ^ at) for peer in range(parts * PAIR)]
        chunks[at] = lax.ppermute(chunk, ("spec", "pair"), pairs)

    held = []
    for turn in reversed(range(parts)):
        same, cross, *held = advect(turn, fields, plan, held, parts, rows, columns)
        send(cross, turn * PAIR + 1)
        held.append(same)
    for turn, chunk in zip(reversed(range(1, parts)), held):
        send(chunk, turn * PAIR)
    chunks[0] = held[-1]
    return chemistry(chunks, take, net, rates, plan)


def solution(mesh):
    shape = (mesh.shape["spec"], mesh.shape["lat"] // PAIR, PAIR)
    inner = Mesh(mesh.devices.reshape(shape), ("spec", "band", "pair"))
    lat = ("band", "pair")
    in_specs = (P("spec", lat, None), P(lat, None), P(), P(), P(), P(), P())
    out_specs = P(None, lat, "spec")

    return jax.shard_map(on_device, mesh=inner, in_specs=in_specs, out_specs=out_specs, check_vma=False)
```

profile of v0, /device:TPU:0, one launch (start us, length us, event | category | flops | bytes accessed | tf_op | source)
XLA Modules:
  0.0 37.0 jit_solution(533612604607076374)
XLA Ops:
  0.0 0.0 copy-start.1
  0.0 0.0 copy-start.2
  0.0 1.1 %pack.1 = (f32[528,128]{1,0:T(8,128)S(1)}, f32[528,128]{1,0:T(8,128)S(1)}) custom-call(f32[1024,128]{1,0:T(8,128)} %bitcast.17, f32[16,128]{1,0:T(8,128)} %bitcast.18), custom_call_target="tpu_custom_call" | custom-call | tf_op jit(solution)/shard_map/pack/pallas_call | solution.py:139
  1.1 0.0 copy-start
  1.1 3.0 %collective-permute-start = (f32[528,128]{1,0:T(8,128)S(1)}, f32[528,128]{1,0:T(8,128)S(1)}, u32[]{:S(2)}, u32[]{:S(2)}) collective-permute-start(f32[528,128]{1,0:T(8,128)S(1)} %get-tuple-element.26), channel_id=1, source_target_pairs={{0,1},{1,0},{2,3},{3,2},{4,5},{5,4},{6,7},{7,6},{8,9},{9,8},{10,11... | collective-permute-start | bytes 811016 | tf_op jit(solution)/shard_map/ppermute | solution.py:336
  4.2 0.7 %collective-permute-start.2 = (f32[528,128]{1,0:T(8,128)S(1)}, f32[528,128]{1,0:T(8,128)S(1)}, u32[]{:S(2)}, u32[]{:S(2)}) collective-permute-start(f32[528,128]{1,0:T(8,128)S(1)} %get-tuple-element.25.own_ref), channel_id=1, source_target_pairs={{2,4},{4,2},{3,5},{5,3},{10,12},{12,10},{11,13},{13,11},{18,20},{2... | collective-permute-start | bytes 811016 | tf_op jit(solution)/shard_map/ppermute | solution.py:338
  4.8 4.4 %collective-permute-start.1 = (f32[528,128]{1,0:T(8,128)S(1)}, f32[528,128]{1,0:T(8,128)S(1)}, u32[]{:S(2)}, u32[]{:S(2)}) collective-permute-start(f32[528,128]{1,0:T(8,128)S(1)} %get-tuple-element.25.own_ref), channel_id=1, source_target_pairs={{0,2},{2,0},{4,6},{6,4},{1,3},{3,1},{5,7},{7,5},{8,10},{10,8},{12,... | collective-permute-start | bytes 811016 | tf_op jit(solution)/shard_map/ppermute | solution.py:337
  9.3 1.4 %collective-permute-done.swap_ref = f32[528,128]{1,0:T(8,128)S(1)} collective-permute-done((f32[528,128]{1,0:T(8,128)S(1)}, f32[528,128]{1,0:T(8,128)S(1)}, u32[]{:S(2)}, u32[]{:S(2)}) %collective-permute-start) | collective-permute-done | bytes 270368 | tf_op jit(solution)/shard_map/ppermute | solution.py:336
  10.6 0.7 %collective-permute-start.4 = (f32[528,128]{1,0:T(8,128)S(1)}, f32[528,128]{1,0:T(8,128)S(1)}, u32[]{:S(2)}, u32[]{:S(2)}) collective-permute-start(f32[528,128]{1,0:T(8,128)S(1)} %collective-permute-done.swap_ref), channel_id=1, source_target_pairs={{2,4},{4,2},{3,5},{5,3},{10,12},{12,10},{11,13},{13,11},{18,20},{2... | collective-permute-start | bytes 811016 | tf_op jit(solution)/shard_map/ppermute | solution.py:340
  11.3 4.7 %collective-permute-start.3 = (f32[528,128]{1,0:T(8,128)S(1)}, f32[528,128]{1,0:T(8,128)S(1)}, u32[]{:S(2)}, u32[]{:S(2)}) collective-permute-start(f32[528,128]{1,0:T(8,128)S(1)} %collective-permute-done.swap_ref), channel_id=1, source_target_pairs={{0,2},{2,0},{4,6},{6,4},{1,3},{3,1},{5,7},{7,5},{8,10},{10,8},{12,... | collective-permute-start | bytes 811016 | tf_op jit(solution)/shard_map/ppermute | solution.py:339
  16.0 0.0 copy-start.3
  16.0 0.0 copy-start.4
  16.0 0.0 copy-done.1
  16.0 0.0 copy-done.2
  16.0 0.0 copy-done
  16.0 0.6 %copy-done.3 = s32[32]{0:T(128)S(1)} copy-done((s32[32]{0:T(128)S(1)}, s32[32]{0:T(128)}, u32[]{:S(2)}) %copy-start.3) | copy-done | bytes 152
  16.7 0.0 copy-done.4
  16.7 2.2 %tables.1 = (bf16[2,1024,256]{2,1,0:T(8,128)(2,1)S(1)}, bf16[256,1024]{1,0:T(8,128)(2,1)S(1)}, f32[1024,128]{1,0:T(8,128)S(1)}, s32[12]{0:T(128)S(1)}) custom-call(s32[2,1024]{1,0:T(2,128)S(1)} %bitcast.14, s32[2,1024]{1,0:T(2,128)S(1)} %bitcast.15, f32[8,128]{1,0:T(8,128)S(1)} %bitcast.16, s32[32]{0:T(128)S(1)} %copy-done.3, s32[32]{0:T(128)S(1)} %copy-done.4), custom_call_target="tpu_custom_call" | custom-call | flops 20000000 | bytes 2000000 | tf_op jit(solution)/shard_map/tables/pallas_call | solution.py:53
  18.9 0.0 collective-permute-done.2.own_b
  18.9 0.0 collective-permute-done.1.own_a
  18.9 0.0 collective-permute-done.4.swap_b
  18.9 2.5 %collective-permute-done.3.swap_a = f32[528,128]{1,0:T(8,128)S(1)} collective-permute-done((f32[528,128]{1,0:T(8,128)S(1)}, f32[528,128]{1,0:T(8,128)S(1)}, u32[]{:S(2)}, u32[]{:S(2)}) %collective-permute-start.3) | collective-permute-done | bytes 270368 | tf_op jit(solution)/shard_map/ppermute | solution.py:339
  21.4 0.6 %shard_map.73 = (f32[4,32,128]{2,1,0:T(8,128)S(1)}, f32[4,32,128]{2,1,0:T(8,128)S(1)}) custom-call(f32[528,128]{1,0:T(8,128)S(1)} %get-tuple-element.25.own_ref, f32[528,128]{1,0:T(8,128)S(1)} %collective-permute-done.swap_ref, f32[528,128]{1,0:T(8,128)S(1)} %collective-permute-done.1.own_a, f32[528,128]{1,0:T(8,128)S(1)} %collective-permute-done.2.own_b, ...), custom_call_target="tpu_custom_call" | custom-call | flops 4000000 | bytes 400000 | tf_op jit(solution)/shard_map/pallas_call | solution.py:238
  21.9 0.2 collective-permute-start.11
  22.2 0.6 %shard_map.74 = (f32[4,32,128]{2,1,0:T(8,128)S(1)}, f32[4,32,128]{2,1,0:T(8,128)S(1)}, f32[4,32,128]{2,1,0:T(8,128)S(1)}) custom-call(f32[528,128]{1,0:T(8,128)S(1)} %get-tuple-element.25.own_ref, f32[528,128]{1,0:T(8,128)S(1)} %collective-permute-done.swap_ref, f32[528,128]{1,0:T(8,128)S(1)} %collective-permute-done.1.own_a, ...), custom_call_target="tpu_custom_call", output_to_operand_aliasing={{2}: (7, {})} | custom-call | flops 4000000 | bytes 400000 | tf_op jit(solution)/shard_map/pallas_call | solution.py:238
  22.7 2.4 %collective-permute-start.9 = (f32[4,32,128]{2,1,0:T(8,128)S(1)}, f32[4,32,128]{2,1,0:T(8,128)S(1)}, u32[]{:S(2)}, u32[]{:S(2)}) collective-permute-start(f32[4,32,128]{2,1,0:T(8,128)S(1)} %get-tuple-element.39), channel_id=1, source_target_pairs={{0,17},{1,16},{8,25},{9,24},{16,1},{17,0},{24,9},{25,8},{2,19},{3,... | collective-permute-start | bytes 196616 | tf_op jit(solution)/shard_map/ppermute | solution.py:349
  25.1 0.6 %shard_map.75 = (f32[4,32,128]{2,1,0:T(8,128)S(1)}, f32[4,32,128]{2,1,0:T(8,128)S(1)}, f32[4,32,128]{2,1,0:T(8,128)S(1)}, f32[4,32,128]{2,1,0:T(8,128)S(1)}) custom-call(f32[528,128]{1,0:T(8,128)S(1)} %get-tuple-element.25.own_ref, f32[528,128]{1,0:T(8,128)S(1)} %collective-permute-done.swap_ref, ...), custom_call_target="tpu_custom_call", output_to_operand_aliasing={{2}: (7, {}), {3}: (8, {})} | custom-call | flops 4000000 | bytes 400000 | tf_op jit(solution)/shard_map/pallas_call | solution.py:238
  25.7 0.6 %shard_map.76 = (f32[4,32,128]{2,1,0:T(8,128)S(1)}, f32[4,32,128]{2,1,0:T(8,128)S(1)}, f32[4,32,128]{2,1,0:T(8,128)S(1)}, f32[4,32,128]{2,1,0:T(8,128)S(1)}, f32[4,32,128]{2,1,0:T(8,128)S(1)}) custom-call(f32[528,128]{1,0:T(8,128)S(1)} %get-tuple-element.25.own_ref, ...), custom_call_target="tpu_custom_call", output_to_operand_aliasing={{2}: (7, {}), {3}: (8, {}), {4}: (9, {})} | custom-call | flops 4000000 | bytes 400000 | tf_op jit(solution)/shard_map/pallas_call | solution.py:238
  26.2 0.6 %collective-permute-start.5 = (f32[4,32,128]{2,1,0:T(8,128)S(1)}, f32[4,32,128]{2,1,0:T(8,128)S(1)}, u32[]{:S(2)}, u32[]{:S(2)}) collective-permute-start(f32[4,32,128]{2,1,0:T(8,128)S(1)} %get-tuple-element.35), channel_id=1, source_target_pairs={{0,1},{1,0},{8,9},{9,8},{16,17},{17,16},{24,25},{25,24},{2,3},{3,2... | collective-permute-start | bytes 196616 | tf_op jit(solution)/shard_map/ppermute | solution.py:349
  26.8 1.0 %collective-permute-start.6 = (f32[4,32,128]{2,1,0:T(8,128)S(1)}, f32[4,32,128]{2,1,0:T(8,128)S(1)}, u32[]{:S(2)}, u32[]{:S(2)}) collective-permute-start(f32[4,32,128]{2,1,0:T(8,128)S(1)} %get-tuple-element.36), channel_id=1, source_target_pairs={{0,8},{1,9},{8,0},{9,1},{16,24},{17,25},{24,16},{25,17},{2,10},{3,... | collective-permute-start | bytes 196616 | tf_op jit(solution)/shard_map/ppermute | solution.py:349
  27.8 1.5 %collective-permute-start.8 = (f32[4,32,128]{2,1,0:T(8,128)S(1)}, f32[4,32,128]{2,1,0:T(8,128)S(1)}, u32[]{:S(2)}, u32[]{:S(2)}) collective-permute-start(f32[4,32,128]{2,1,0:T(8,128)S(1)} %get-tuple-element.38), channel_id=1, source_target_pairs={{0,16},{1,17},{8,24},{9,25},{16,0},{17,1},{24,8},{25,9},{2,18},{3,... | collective-permute-start | bytes 196616 | tf_op jit(solution)/shard_map/ppermute | solution.py:349
  29.3 0.0 collective-permute-done.11.refs_7_
  29.3 0.0 collective-permute-start.10
  29.3 0.0 collective-permute-done.9.refs_5_
  29.3 0.8 %collective-permute-start.7 = (f32[4,32,128]{2,1,0:T(8,128)S(1)}, f32[4,32,128]{2,1,0:T(8,128)S(1)}, u32[]{:S(2)}, u32[]{:S(2)}) collective-permute-start(f32[4,32,128]{2,1,0:T(8,128)S(1)} %get-tuple-element.37), channel_id=1, source_target_pairs={{0,9},{1,8},{8,1},{9,0},{16,25},{17,24},{24,17},{25,16},{2,11},{3,... | collective-permute-start | bytes 196616 | tf_op jit(solution)/shard_map/ppermute | solution.py:349
  30.1 0.5 %collective-permute-done.5.refs_1_ = f32[4,32,128]{2,1,0:T(8,128)S(1)} collective-permute-done((f32[4,32,128]{2,1,0:T(8,128)S(1)}, f32[4,32,128]{2,1,0:T(8,128)S(1)}, u32[]{:S(2)}, u32[]{:S(2)}) %collective-permute-start.5) | collective-permute-done | bytes 65568 | tf_op jit(solution)/shard_map/ppermute | solution.py:349
  30.6 0.0 collective-permute-done.6.refs_2_
  30.6 1.5 %collective-permute-done.8.refs_4_ = f32[4,32,128]{2,1,0:T(8,128)S(1)} collective-permute-done((f32[4,32,128]{2,1,0:T(8,128)S(1)}, f32[4,32,128]{2,1,0:T(8,128)S(1)}, u32[]{:S(2)}, u32[]{:S(2)}) %collective-permute-start.8) | collective-permute-done | bytes 65568 | tf_op jit(solution)/shard_map/ppermute | solution.py:349
  32.1 1.6 %collective-permute-done.10.refs_6_ = f32[4,32,128]{2,1,0:T(8,128)S(1)} collective-permute-done((f32[4,32,128]{2,1,0:T(8,128)S(1)}, f32[4,32,128]{2,1,0:T(8,128)S(1)}, u32[]{:S(2)}, u32[]{:S(2)}) %collective-permute-start.10) | collective-permute-done | bytes 65568 | tf_op jit(solution)/shard_map/ppermute | solution.py:349
  33.6 0.0 collective-permute-done.7.refs_3_
  33.6 3.4 %chemistry.1 = f32[1024,128]{1,0:T(8,128)} custom-call(f32[4,32,128]{2,1,0:T(8,128)S(1)} %get-tuple-element.34.refs_0_, f32[4,32,128]{2,1,0:T(8,128)S(1)} %collective-permute-done.5.refs_1_, f32[4,32,128]{2,1,0:T(8,128)S(1)} %collective-permute-done.6.refs_2_, f32[4,32,128]{2,1,0:T(8,128)S(1)} %collective-permute-done.7.refs_3_, ...), custom_call_target="tpu_custom_call" | custom-call | tf_op jit(solution)/shard_map/chemistry/pallas_call | solution.py:308
Async XLA Ops:
  0.0 16.0 %copy-start.1 = (s32[1024,2]{0,1:T(2,128)S(1)}, s32[1024,2]{0,1:T(2,128)}, u32[]{:S(2)}) copy-start(s32[1024,2]{0,1:T(2,128)} %param.11) | copy-start | bytes 24580
  0.0 16.0 %copy-start.2 = (f32[1024]{0:T(1024)S(1)}, f32[1024]{0:T(1024)}, u32[]{:S(2)}) copy-start(f32[1024]{0:T(1024)} %param.9) | copy-start | bytes 12292
  1.1 14.9 %copy-start = (s32[1024,2]{0,1:T(2,128)S(1)}, s32[1024,2]{0,1:T(2,128)}, u32[]{:S(2)}) copy-start(s32[1024,2]{0,1:T(2,128)} %param.10) | copy-start | bytes 24580
  1.1 9.5 %collective-permute-start = (f32[528,128]{1,0:T(8,128)S(1)}, f32[528,128]{1,0:T(8,128)S(1)}, u32[]{:S(2)}, u32[]{:S(2)}) collective-permute-start(f32[528,128]{1,0:T(8,128)S(1)} %get-tuple-element.26), channel_id=1, source_target_pairs={{0,1},{1,0},{2,3},{3,2},{4,5},{5,4},{6,7},{7,6},{8,9},{9,8},{10,11... | collective-permute-start | bytes 811016 | tf_op jit(solution)/shard_map/ppermute | solution.py:336
  4.2 14.7 %collective-permute-start.2 = (f32[528,128]{1,0:T(8,128)S(1)}, f32[528,128]{1,0:T(8,128)S(1)}, u32[]{:S(2)}, u32[]{:S(2)}) collective-permute-start(f32[528,128]{1,0:T(8,128)S(1)} %get-tuple-element.25.own_ref), channel_id=1, source_target_pairs={{2,4},{4,2},{3,5},{5,3},{10,12},{12,10},{11,13},{13,11},{18,20},{2... | collective-permute-start | bytes 811016 | tf_op jit(solution)/shard_map/ppermute | solution.py:338
  4.8 14.1 %collective-permute-start.1 = (f32[528,128]{1,0:T(8,128)S(1)}, f32[528,128]{1,0:T(8,128)S(1)}, u32[]{:S(2)}, u32[]{:S(2)}) collective-permute-start(f32[528,128]{1,0:T(8,128)S(1)} %get-tuple-element.25.own_ref), channel_id=1, source_target_pairs={{0,2},{2,0},{4,6},{6,4},{1,3},{3,1},{5,7},{7,5},{8,10},{10,8},{12,... | collective-permute-start | bytes 811016 | tf_op jit(solution)/shard_map/ppermute | solution.py:337
  10.6 8.3 %collective-permute-start.4 = (f32[528,128]{1,0:T(8,128)S(1)}, f32[528,128]{1,0:T(8,128)S(1)}, u32[]{:S(2)}, u32[]{:S(2)}) collective-permute-start(f32[528,128]{1,0:T(8,128)S(1)} %collective-permute-done.swap_ref), channel_id=1, source_target_pairs={{2,4},{4,2},{3,5},{5,3},{10,12},{12,10},{11,13},{13,11},{18,20},{2... | collective-permute-start | bytes 811016 | tf_op jit(solution)/shard_map/ppermute | solution.py:340
  11.3 10.0 %collective-permute-start.3 = (f32[528,128]{1,0:T(8,128)S(1)}, f32[528,128]{1,0:T(8,128)S(1)}, u32[]{:S(2)}, u32[]{:S(2)}) collective-permute-start(f32[528,128]{1,0:T(8,128)S(1)} %collective-permute-done.swap_ref), channel_id=1, source_target_pairs={{0,2},{2,0},{4,6},{6,4},{1,3},{3,1},{5,7},{7,5},{8,10},{10,8},{12,... | collective-permute-start | bytes 811016 | tf_op jit(solution)/shard_map/ppermute | solution.py:339
  16.0 0.7 %copy-start.3 = (s32[32]{0:T(128)S(1)}, s32[32]{0:T(128)}, u32[]{:S(2)}) copy-start(s32[32]{0:T(128)} %slot_ref.1) | copy-start | bytes 388
  16.0 0.7 %copy-start.4 = (s32[32]{0:T(128)S(1)}, s32[32]{0:T(128)}, u32[]{:S(2)}) copy-start(s32[32]{0:T(128)} %day_ref.1) | copy-start | bytes 388
  21.9 7.4 %collective-permute-start.11 = (f32[4,32,128]{2,1,0:T(8,128)S(1)}, f32[4,32,128]{2,1,0:T(8,128)S(1)}, u32[]{:S(2)}, u32[]{:S(2)}) collective-permute-start(f32[4,32,128]{2,1,0:T(8,128)S(1)} %get-tuple-element.41), channel_id=1, source_target_pairs={{0,25},{1,24},{8,17},{9,16},{16,9},{17,8},{24,1},{25,0},{2,27},{3,... | collective-permute-start | bytes 196616 | tf_op jit(solution)/shard_map/ppermute | solution.py:349
  22.7 6.6 %collective-permute-start.9 = (f32[4,32,128]{2,1,0:T(8,128)S(1)}, f32[4,32,128]{2,1,0:T(8,128)S(1)}, u32[]{:S(2)}, u32[]{:S(2)}) collective-permute-start(f32[4,32,128]{2,1,0:T(8,128)S(1)} %get-tuple-element.39), channel_id=1, source_target_pairs={{0,17},{1,16},{8,25},{9,24},{16,1},{17,0},{24,9},{25,8},{2,19},{3,... | collective-permute-start | bytes 196616 | tf_op jit(solution)/shard_map/ppermute | solution.py:349
  26.2 4.4 %collective-permute-start.5 = (f32[4,32,128]{2,1,0:T(8,128)S(1)}, f32[4,32,128]{2,1,0:T(8,128)S(1)}, u32[]{:S(2)}, u32[]{:S(2)}) collective-permute-start(f32[4,32,128]{2,1,0:T(8,128)S(1)} %get-tuple-element.35), channel_id=1, source_target_pairs={{0,1},{1,0},{8,9},{9,8},{16,17},{17,16},{24,25},{25,24},{2,3},{3,2... | collective-permute-start | bytes 196616 | tf_op jit(solution)/shard_map/ppermute | solution.py:349
  26.8 3.8 %collective-permute-start.6 = (f32[4,32,128]{2,1,0:T(8,128)S(1)}, f32[4,32,128]{2,1,0:T(8,128)S(1)}, u32[]{:S(2)}, u32[]{:S(2)}) collective-permute-start(f32[4,32,128]{2,1,0:T(8,128)S(1)} %get-tuple-element.36), channel_id=1, source_target_pairs={{0,8},{1,9},{8,0},{9,1},{16,24},{17,25},{24,16},{25,17},{2,10},{3,... | collective-permute-start | bytes 196616 | tf_op jit(solution)/shard_map/ppermute | solution.py:349
  27.8 4.3 %collective-permute-start.8 = (f32[4,32,128]{2,1,0:T(8,128)S(1)}, f32[4,32,128]{2,1,0:T(8,128)S(1)}, u32[]{:S(2)}, u32[]{:S(2)}) collective-permute-start(f32[4,32,128]{2,1,0:T(8,128)S(1)} %get-tuple-element.38), channel_id=1, source_target_pairs={{0,16},{1,17},{8,24},{9,25},{16,0},{17,1},{24,8},{25,9},{2,18},{3,... | collective-permute-start | bytes 196616 | tf_op jit(solution)/shard_map/ppermute | solution.py:349
  29.3 4.3 %collective-permute-start.10 = (f32[4,32,128]{2,1,0:T(8,128)S(1)}, f32[4,32,128]{2,1,0:T(8,128)S(1)}, u32[]{:S(2)}, u32[]{:S(2)}) collective-permute-start(f32[4,32,128]{2,1,0:T(8,128)S(1)} %get-tuple-element.40), channel_id=1, source_target_pairs={{0,24},{1,25},{8,16},{9,17},{16,8},{17,9},{24,0},{25,1},{2,26},{3,... | collective-permute-start | bytes 196616 | tf_op jit(solution)/shard_map/ppermute | solution.py:349
  29.3 4.3 %collective-permute-start.7 = (f32[4,32,128]{2,1,0:T(8,128)S(1)}, f32[4,32,128]{2,1,0:T(8,128)S(1)}, u32[]{:S(2)}, u32[]{:S(2)}) collective-permute-start(f32[4,32,128]{2,1,0:T(8,128)S(1)} %get-tuple-element.37), channel_id=1, source_target_pairs={{0,9},{1,8},{8,1},{9,0},{16,25},{17,24},{24,17},{25,16},{2,11},{3,... | collective-permute-start | bytes 196616 | tf_op jit(solution)/shard_map/ppermute | solution.py:349
where the time goes:
time: 37.2 us; the launch traced here: 37 us
  starting transfers between devices  20 us (54%)
  Pallas kernels  8.89 us (24%)
  waiting for transfers between devices  7.36 us (20%)
  local copies, waits for them, and re-layouts  0.67 us (2%)
    ppermute x7, starting transfers between devices, send(): chunks[at] = lax.ppermute(chunk, ('spec', 'pair'), pairs)  6.45 us
    ppermute x1, starting transfers between devices, on_device(): swap_a = lax.ppermute(swap, 'band', couples(bands, 0))  4.7 us
    ppermute x1, starting transfers between devices, on_device(): own_a = lax.ppermute(own, 'band', couples(bands, 0))  4.45 us
    ppermute x7, waiting for transfers between devices, send(): chunks[at] = lax.ppermute(chunk, ('spec', 'pair'), pairs)  3.54 us
    pallas_call x1, Pallas kernels, chemistry(): pl.pallas_call(functools.partial(chemistry_kernel, len(chunks)), out_shap...  3.36 us
    ppermute x1, starting transfers between devices, on_device(): swap = lax.ppermute(other, 'pair', couples(PAIR, 0))  3.03 us
    ppermute x1, waiting for transfers between devices, on_device(): swap_a = lax.ppermute(swap, 'band', couples(bands, 0))  2.46 us
    pallas_call x4, Pallas kernels, advect(): pl.pallas_call(functools.partial(advect_kernel, turn, len(held)), out_sha...  2.25 us
  transfers between devices with their start and end apart: 12, of which 5 were waited for; matrix products, arithmetic and copies ran while one was open for 0% of the time, Pallas kernels for 10%

commit v1 on v0

--- a/solution.py
+++ b/solution.py
@@ -148,9 +148,7 @@
 
 
 def minmod(left, right):
-    low = jnp.minimum(left, right)
-    high = jnp.maximum(left, right)
-    return jnp.maximum(low, 0.0) + jnp.minimum(high, 0.0)
+    return jnp.maximum(jnp.minimum(left, right), jnp.minimum(jnp.maximum(left, right), 0.0))
 
 
 def sweep(load, courant, store, first, count):
@@ -165,20 +163,19 @@
         following = load(row + 1)
         step_next = following - here
         slope_here = minmod(step_next, step_here)
-        number = courant(row)
-        up = jnp.maximum(number, 0.0)
-        down = jnp.minimum(number, 0.0)
-        up_half = up * (0.5 * (1.0 - number))
-        down_half = down * (-0.5 * (1.0 + number))
-        flux = (up * old + up_half * slope_old) + (down * here + down_half * slope_here)
+        number = jnp.broadcast_to(courant(row), here.shape)
+        ahead = number > 0.0
+        lean = jnp.where(ahead, 0.5 * (1.0 - number), -0.5 * (1.0 + number))
+        flux = number * (jnp.where(ahead, old, here) + lean * jnp.where(ahead, slope_old, slope_here))
         if flux_old is not None:
             store(row - 1, old - (flux - flux_old))
         old, here, step_here, slope_old, flux_old = here, following, step_next, slope_here, flux
 
 
-def advect_kernel(turn, held, own_ref, swap_ref, own_a, own_b, swap_a, swap_b, plan_ref, *refs):
-    same_ref, cross_ref = refs[held : held + 2]
-    window, flow, middle, advected, plan, sem = refs[2 * held + 2 :]
+def advect_kernel(
+    turn, own_ref, swap_ref, own_a, own_b, swap_a, swap_b, plan_ref, same_ref, cross_ref,
+    window, flow, middle, advected, plan, sem,
+):
     fetch = pltpu.make_async_copy(plan_ref, plan, sem)
     fetch.start()
     rows, species, width = same_ref.shape
@@ -230,17 +227,16 @@
         cross_ref[place] = advected[plan[(1 - side) * rows + place]]
 
 
-def advect(turn, fields, plan, held, parts, rows, columns):
+def advect(turn, fields, plan, parts, rows, columns):
     species = fields[0].shape[0] * LANES // (rows * columns) - 1
     span = PAIR * rows
     width = columns // parts
     chunk = jax.ShapeDtypeStruct((rows, species, width), jnp.float32)
     return pl.pallas_call(
-        functools.partial(advect_kernel, turn, len(held)),
-        out_shape=(chunk, chunk) + (chunk,) * len(held),
-        in_specs=[VMEM] * 7 + [pl.BlockSpec(memory_space=pl.ANY)] * len(held),
-        out_specs=(VMEM, VMEM) + (pl.BlockSpec(memory_space=pl.ANY),) * len(held),
-        input_output_aliases={7 + at: 2 + at for at in range(len(held))},
+        functools.partial(advect_kernel, turn),
+        out_shape=(chunk, chunk),
+        in_specs=[VMEM] * 7,
+        out_specs=(VMEM, VMEM),
         scratch_shapes=[
             pltpu.VMEM((3 * span, species, width), jnp.float32),
             pltpu.VMEM((3 * span, 1, width), jnp.float32),
@@ -251,7 +247,7 @@
         ],
         compiler_params=params(8),
         cost_estimate=pl.CostEstimate(flops=4_000_000, bytes_accessed=400_000, transcendentals=0),
-    )(*fields, plan, *held)
+    )(*fields, plan)
 
 
 def split_rows(value):
@@ -348,14 +344,12 @@
         pairs = [(peer, peer ^ at) for peer in range(parts * PAIR)]
         chunks[at] = lax.ppermute(chunk, ("spec", "pair"), pairs)
 
-    held = []
     for turn in reversed(range(parts)):
-        same, cross, *held = advect(turn, fields, plan, held, parts, rows, columns)
+        same, cross = advect(turn, fields, plan, parts, rows, columns)
         send(cross, turn * PAIR + 1)
-        held.append(same)
-    for turn, chunk in zip(reversed(range(1, parts)), held):
-        send(chunk, turn * PAIR)
-    chunks[0] = held[-1]
+        if turn:
+            send(same, turn * PAIR)
+    chunks[0] = same
     return chemistry(chunks, take, net, rates, plan)
 
 

time: 37.2 us -> 38 us (1.022)
  starting transfers between devices: 20 us -> 20.6 us
    ppermute x7, starting transfers between devices: 6.45 us -> 7.05 us  [send(): chunks[at] = lax.ppermute(chunk, ('spec', 'pair'), pairs)]
where the time goes in v1:
time: 38 us; the launch traced here: 37.8 us
  starting transfers between devices  20.6 us (54%)
  Pallas kernels  8.9 us (23%)
  waiting for transfers between devices  7.56 us (20%)
  local copies, waits for them, and re-layouts  0.67 us (2%)
    ppermute x7, starting transfers between devices, send(): chunks[at] = lax.ppermute(chunk, ('spec', 'pair'), pairs)  7.05 us
    ppermute x1, starting transfers between devices, on_device(): swap_a = lax.ppermute(swap, 'band', couples(bands, 0))  4.7 us
    ppermute x1, starting transfers between devices, on_device(): own_a = lax.ppermute(own, 'band', couples(bands, 0))  4.45 us
    ppermute x7, waiting for transfers between devices, send(): chunks[at] = lax.ppermute(chunk, ('spec', 'pair'), pairs)  3.73 us
    pallas_call x1, Pallas kernels, chemistry(): pl.pallas_call(functools.partial(chemistry_kernel, len(chunks)), out_shap...  3.37 us
    ppermute x1, starting transfers between devices, on_device(): swap = lax.ppermute(other, 'pair', couples(PAIR, 0))  3.03 us
    ppermute x1, waiting for transfers between devices, on_device(): swap_a = lax.ppermute(swap, 'band', couples(bands, 0))  2.46 us
    pallas_call x4, Pallas kernels, advect(): pl.pallas_call(functools.partial(advect_kernel, turn), out_shape=(chunk,...  2.25 us
  transfers between devices with their start and end apart: 12, of which 5 were waited for; matrix products, arithmetic and copies ran while one was open for 0% of the time, Pallas kernels for 10%

profile of v1, /device:TPU:0, one launch (start us, length us, event | category | flops | bytes accessed | tf_op | source)
XLA Modules:
  0.0 37.8 jit_solution(16463556443542728881)
XLA Ops:
  0.0 0.0 copy-start.1
  0.0 0.0 copy-start.2
  0.0 1.1 %pack.1 = (f32[528,128]{1,0:T(8,128)S(1)}, f32[528,128]{1,0:T(8,128)S(1)}) custom-call(f32[1024,128]{1,0:T(8,128)} %bitcast.17, f32[16,128]{1,0:T(8,128)} %bitcast.18), custom_call_target="tpu_custom_call" | custom-call | tf_op jit(solution)/shard_map/pack/pallas_call | solution.py:139
  1.1 0.0 copy-start
  1.1 3.0 %collective-permute-start = (f32[528,128]{1,0:T(8,128)S(1)}, f32[528,128]{1,0:T(8,128)S(1)}, u32[]{:S(2)}, u32[]{:S(2)}) collective-permute-start(f32[528,128]{1,0:T(8,128)S(1)} %get-tuple-element.20), channel_id=1, source_target_pairs={{0,1},{1,0},{2,3},{3,2},{4,5},{5,4},{6,7},{7,6},{8,9},{9,8},{10,11... | collective-permute-start | bytes 811016 | tf_op jit(solution)/shard_map/ppermute | solution.py:332
  4.2 0.7 %collective-permute-start.2 = (f32[528,128]{1,0:T(8,128)S(1)}, f32[528,128]{1,0:T(8,128)S(1)}, u32[]{:S(2)}, u32[]{:S(2)}) collective-permute-start(f32[528,128]{1,0:T(8,128)S(1)} %get-tuple-element.19.own_ref), channel_id=1, source_target_pairs={{2,4},{4,2},{3,5},{5,3},{10,12},{12,10},{11,13},{13,11},{18,20},{2... | collective-permute-start | bytes 811016 | tf_op jit(solution)/shard_map/ppermute | solution.py:334
  4.8 4.4 %collective-permute-start.1 = (f32[528,128]{1,0:T(8,128)S(1)}, f32[528,128]{1,0:T(8,128)S(1)}, u32[]{:S(2)}, u32[]{:S(2)}) collective-permute-start(f32[528,128]{1,0:T(8,128)S(1)} %get-tuple-element.19.own_ref), channel_id=1, source_target_pairs={{0,2},{2,0},{4,6},{6,4},{1,3},{3,1},{5,7},{7,5},{8,10},{10,8},{12,... | collective-permute-start | bytes 811016 | tf_op jit(solution)/shard_map/ppermute | solution.py:333
  9.3 1.4 %collective-permute-done.swap_ref = f32[528,128]{1,0:T(8,128)S(1)} collective-permute-done((f32[528,128]{1,0:T(8,128)S(1)}, f32[528,128]{1,0:T(8,128)S(1)}, u32[]{:S(2)}, u32[]{:S(2)}) %collective-permute-start) | collective-permute-done | bytes 270368 | tf_op jit(solution)/shard_map/ppermute | solution.py:332
  10.6 0.7 %collective-permute-start.4 = (f32[528,128]{1,0:T(8,128)S(1)}, f32[528,128]{1,0:T(8,128)S(1)}, u32[]{:S(2)}, u32[]{:S(2)}) collective-permute-start(f32[528,128]{1,0:T(8,128)S(1)} %collective-permute-done.swap_ref), channel_id=1, source_target_pairs={{2,4},{4,2},{3,5},{5,3},{10,12},{12,10},{11,13},{13,11},{18,20},{2... | collective-permute-start | bytes 811016 | tf_op jit(solution)/shard_map/ppermute | solution.py:336
  11.3 4.7 %collective-permute-start.3 = (f32[528,128]{1,0:T(8,128)S(1)}, f32[528,128]{1,0:T(8,128)S(1)}, u32[]{:S(2)}, u32[]{:S(2)}) collective-permute-start(f32[528,128]{1,0:T(8,128)S(1)} %collective-permute-done.swap_ref), channel_id=1, source_target_pairs={{0,2},{2,0},{4,6},{6,4},{1,3},{3,1},{5,7},{7,5},{8,10},{10,8},{12,... | collective-permute-start | bytes 811016 | tf_op jit(solution)/shard_map/ppermute | solution.py:335
  16.0 0.0 copy-start.3
  16.0 0.0 copy-start.4
  16.0 0.0 copy-done.1
  16.0 0.0 copy-done.2
  16.0 0.0 copy-done
  16.0 0.6 %copy-done.3 = s32[32]{0:T(128)S(1)} copy-done((s32[32]{0:T(128)S(1)}, s32[32]{0:T(128)}, u32[]{:S(2)}) %copy-start.3) | copy-done | bytes 152
  16.7 0.0 copy-done.4
  16.7 2.2 %tables.1 = (bf16[2,1024,256]{2,1,0:T(8,128)(2,1)S(1)}, bf16[256,1024]{1,0:T(8,128)(2,1)S(1)}, f32[1024,128]{1,0:T(8,128)S(1)}, s32[12]{0:T(128)S(1)}) custom-call(s32[2,1024]{1,0:T(2,128)S(1)} %bitcast.14, s32[2,1024]{1,0:T(2,128)S(1)} %bitcast.15, f32[8,128]{1,0:T(8,128)S(1)} %bitcast.16, s32[32]{0:T(128)S(1)} %copy-done.3, s32[32]{0:T(128)S(1)} %copy-done.4), custom_call_target="tpu_custom_call" | custom-call | flops 20000000 | bytes 2000000 | tf_op jit(solution)/shard_map/tables/pallas_call | solution.py:53
  18.9 0.0 collective-permute-done.2.own_b
  18.9 0.0 collective-permute-done.1.own_a
  18.9 0.0 collective-permute-done.4.swap_b
  18.9 2.5 %collective-permute-done.3.swap_a = f32[528,128]{1,0:T(8,128)S(1)} collective-permute-done((f32[528,128]{1,0:T(8,128)S(1)}, f32[528,128]{1,0:T(8,128)S(1)}, u32[]{:S(2)}, u32[]{:S(2)}) %collective-permute-start.3) | collective-permute-done | bytes 270368 | tf_op jit(solution)/shard_map/ppermute | solution.py:335
  21.4 0.6 %shard_map.76 = (f32[4,32,128]{2,1,0:T(8,128)S(1)}, f32[4,32,128]{2,1,0:T(8,128)S(1)}) custom-call(f32[528,128]{1,0:T(8,128)S(1)} %get-tuple-element.19.own_ref, f32[528,128]{1,0:T(8,128)S(1)} %collective-permute-done.swap_ref, f32[528,128]{1,0:T(8,128)S(1)} %collective-permute-done.1.own_a, f32[528,128]{1,0:T(8,128)S(1)} %collective-permute-done.2.own_b, ...), custom_call_target="tpu_custom_call" | custom-call | flops 4000000 | bytes 400000 | tf_op jit(solution)/shard_map/pallas_call | solution.py:235
  21.9 0.1 collective-permute-start.10
  22.0 2.7 %collective-permute-start.11 = (f32[4,32,128]{2,1,0:T(8,128)S(1)}, f32[4,32,128]{2,1,0:T(8,128)S(1)}, u32[]{:S(2)}, u32[]{:S(2)}) collective-permute-start(f32[4,32,128]{2,1,0:T(8,128)S(1)} %get-tuple-element.29), channel_id=1, source_target_pairs={{0,25},{1,24},{8,17},{9,16},{16,9},{17,8},{24,1},{25,0},{2,27},{3,... | collective-permute-start | bytes 196616 | tf_op jit(solution)/shard_map/ppermute | solution.py:345
  24.7 0.6 %shard_map.75 = (f32[4,32,128]{2,1,0:T(8,128)S(1)}, f32[4,32,128]{2,1,0:T(8,128)S(1)}) custom-call(f32[528,128]{1,0:T(8,128)S(1)} %get-tuple-element.19.own_ref, f32[528,128]{1,0:T(8,128)S(1)} %collective-permute-done.swap_ref, f32[528,128]{1,0:T(8,128)S(1)} %collective-permute-done.1.own_a, f32[528,128]{1,0:T(8,128)S(1)} %collective-permute-done.2.own_b, ...), custom_call_target="tpu_custom_call" | custom-call | flops 4000000 | bytes 400000 | tf_op jit(solution)/shard_map/pallas_call | solution.py:235
  25.2 1.6 %collective-permute-start.8 = (f32[4,32,128]{2,1,0:T(8,128)S(1)}, f32[4,32,128]{2,1,0:T(8,128)S(1)}, u32[]{:S(2)}, u32[]{:S(2)}) collective-permute-start(f32[4,32,128]{2,1,0:T(8,128)S(1)} %get-tuple-element.26), channel_id=1, source_target_pairs={{0,16},{1,17},{8,24},{9,25},{16,0},{17,1},{24,8},{25,9},{2,18},{3,... | collective-permute-start | bytes 196616 | tf_op jit(solution)/shard_map/ppermute | solution.py:345
  26.8 0.5 %collective-permute-start.9 = (f32[4,32,128]{2,1,0:T(8,128)S(1)}, f32[4,32,128]{2,1,0:T(8,128)S(1)}, u32[]{:S(2)}, u32[]{:S(2)}) collective-permute-start(f32[4,32,128]{2,1,0:T(8,128)S(1)} %get-tuple-element.27), channel_id=1, source_target_pairs={{0,17},{1,16},{8,25},{9,24},{16,1},{17,0},{24,9},{25,8},{2,19},{3,... | collective-permute-start | bytes 196616 | tf_op jit(solution)/shard_map/ppermute | solution.py:345
  27.3 0.6 %shard_map.74 = (f32[4,32,128]{2,1,0:T(8,128)S(1)}, f32[4,32,128]{2,1,0:T(8,128)S(1)}) custom-call(f32[528,128]{1,0:T(8,128)S(1)} %get-tuple-element.19.own_ref, f32[528,128]{1,0:T(8,128)S(1)} %collective-permute-done.swap_ref, f32[528,128]{1,0:T(8,128)S(1)} %collective-permute-done.1.own_a, f32[528,128]{1,0:T(8,128)S(1)} %collective-permute-done.2.own_b, ...), custom_call_target="tpu_custom_call" | custom-call | flops 4000000 | bytes 400000 | tf_op jit(solution)/shard_map/pallas_call | solution.py:235
  27.9 0.1 collective-permute-start.6
  28.0 0.6 %shard_map.73 = (f32[4,32,128]{2,1,0:T(8,128)S(1)}, f32[4,32,128]{2,1,0:T(8,128)S(1)}) custom-call(f32[528,128]{1,0:T(8,128)S(1)} %get-tuple-element.19.own_ref, f32[528,128]{1,0:T(8,128)S(1)} %collective-permute-done.swap_ref, f32[528,128]{1,0:T(8,128)S(1)} %collective-permute-done.1.own_a, f32[528,128]{1,0:T(8,128)S(1)} %collective-permute-done.2.own_b, ...), custom_call_target="tpu_custom_call" | custom-call | flops 4000000 | bytes 400000 | tf_op jit(solution)/shard_map/pallas_call | solution.py:235
  28.5 0.0 collective-permute-done.10.refs_6_
  28.5 1.7 %collective-permute-start.7 = (f32[4,32,128]{2,1,0:T(8,128)S(1)}, f32[4,32,128]{2,1,0:T(8,128)S(1)}, u32[]{:S(2)}, u32[]{:S(2)}) collective-permute-start(f32[4,32,128]{2,1,0:T(8,128)S(1)} %get-tuple-element.25), channel_id=1, source_target_pairs={{0,9},{1,8},{8,1},{9,0},{16,25},{17,24},{24,17},{25,16},{2,11},{3,... | collective-permute-start | bytes 196616 | tf_op jit(solution)/shard_map/ppermute | solution.py:345
  30.2 0.0 collective-permute-done.11.refs_7_
  30.2 0.5 %collective-permute-start.5 = (f32[4,32,128]{2,1,0:T(8,128)S(1)}, f32[4,32,128]{2,1,0:T(8,128)S(1)}, u32[]{:S(2)}, u32[]{:S(2)}) collective-permute-start(f32[4,32,128]{2,1,0:T(8,128)S(1)} %get-tuple-element.23), channel_id=1, source_target_pairs={{0,1},{1,0},{8,9},{9,8},{16,17},{17,16},{24,25},{25,24},{2,3},{3,2... | collective-permute-start | bytes 196616 | tf_op jit(solution)/shard_map/ppermute | solution.py:345
  30.7 0.0 collective-permute-done.8.refs_4_
  30.7 1.3 %collective-permute-done.9.refs_5_ = f32[4,32,128]{2,1,0:T(8,128)S(1)} collective-permute-done((f32[4,32,128]{2,1,0:T(8,128)S(1)}, f32[4,32,128]{2,1,0:T(8,128)S(1)}, u32[]{:S(2)}, u32[]{:S(2)}) %collective-permute-start.9) | collective-permute-done | bytes 65568 | tf_op jit(solution)/shard_map/ppermute | solution.py:345
  32.0 0.0 collective-permute-done.6.refs_2_
  32.0 0.7 %collective-permute-done.7.refs_3_ = f32[4,32,128]{2,1,0:T(8,128)S(1)} collective-permute-done((f32[4,32,128]{2,1,0:T(8,128)S(1)}, f32[4,32,128]{2,1,0:T(8,128)S(1)}, u32[]{:S(2)}, u32[]{:S(2)}) %collective-permute-start.7) | collective-permute-done | bytes 65568 | tf_op jit(solution)/shard_map/ppermute | solution.py:345
  32.7 1.8 %collective-permute-done.5.refs_1_ = f32[4,32,128]{2,1,0:T(8,128)S(1)} collective-permute-done((f32[4,32,128]{2,1,0:T(8,128)S(1)}, f32[4,32,128]{2,1,0:T(8,128)S(1)}, u32[]{:S(2)}, u32[]{:S(2)}) %collective-permute-start.5) | collective-permute-done | bytes 65568 | tf_op jit(solution)/shard_map/ppermute | solution.py:345
  34.5 3.4 %chemistry.1 = f32[1024,128]{1,0:T(8,128)} custom-call(f32[4,32,128]{2,1,0:T(8,128)S(1)} %get-tuple-element.22.refs_0_, f32[4,32,128]{2,1,0:T(8,128)S(1)} %collective-permute-done.5.refs_1_, f32[4,32,128]{2,1,0:T(8,128)S(1)} %collective-permute-done.6.refs_2_, f32[4,32,128]{2,1,0:T(8,128)S(1)} %collective-permute-done.7.refs_3_, ...), custom_call_target="tpu_custom_call" | custom-call | tf_op jit(solution)/shard_map/chemistry/pallas_call | solution.py:304
Async XLA Ops:
  0.0 16.0 %copy-start.1 = (s32[1024,2]{0,1:T(2,128)S(1)}, s32[1024,2]{0,1:T(2,128)}, u32[]{:S(2)}) copy-start(s32[1024,2]{0,1:T(2,128)} %param.11) | copy-start | bytes 24580
  0.0 16.0 %copy-start.2 = (f32[1024]{0:T(1024)S(1)}, f32[1024]{0:T(1024)}, u32[]{:S(2)}) copy-start(f32[1024]{0:T(1024)} %param.9) | copy-start | bytes 12292
  1.1 14.9 %copy-start = (s32[1024,2]{0,1:T(2,128)S(1)}, s32[1024,2]{0,1:T(2,128)}, u32[]{:S(2)}) copy-start(s32[1024,2]{0,1:T(2,128)} %param.10) | copy-start | bytes 24580
  1.1 9.5 %collective-permute-start = (f32[528,128]{1,0:T(8,128)S(1)}, f32[528,128]{1,0:T(8,128)S(1)}, u32[]{:S(2)}, u32[]{:S(2)}) collective-permute-start(f32[528,128]{1,0:T(8,128)S(1)} %get-tuple-element.20), channel_id=1, source_target_pairs={{0,1},{1,0},{2,3},{3,2},{4,5},{5,4},{6,7},{7,6},{8,9},{9,8},{10,11... | collective-permute-start | bytes 811016 | tf_op jit(solution)/shard_map/ppermute | solution.py:332
  4.2 14.7 %collective-permute-start.2 = (f32[528,128]{1,0:T(8,128)S(1)}, f32[528,128]{1,0:T(8,128)S(1)}, u32[]{:S(2)}, u32[]{:S(2)}) collective-permute-start(f32[528,128]{1,0:T(8,128)S(1)} %get-tuple-element.19.own_ref), channel_id=1, source_target_pairs={{2,4},{4,2},{3,5},{5,3},{10,12},{12,10},{11,13},{13,11},{18,20},{2... | collective-permute-start | bytes 811016 | tf_op jit(solution)/shard_map/ppermute | solution.py:334
  4.8 14.1 %collective-permute-start.1 = (f32[528,128]{1,0:T(8,128)S(1)}, f32[528,128]{1,0:T(8,128)S(1)}, u32[]{:S(2)}, u32[]{:S(2)}) collective-permute-start(f32[528,128]{1,0:T(8,128)S(1)} %get-tuple-element.19.own_ref), channel_id=1, source_target_pairs={{0,2},{2,0},{4,6},{6,4},{1,3},{3,1},{5,7},{7,5},{8,10},{10,8},{12,... | collective-permute-start | bytes 811016 | tf_op jit(solution)/shard_map/ppermute | solution.py:333
  10.6 8.3 %collective-permute-start.4 = (f32[528,128]{1,0:T(8,128)S(1)}, f32[528,128]{1,0:T(8,128)S(1)}, u32[]{:S(2)}, u32[]{:S(2)}) collective-permute-start(f32[528,128]{1,0:T(8,128)S(1)} %collective-permute-done.swap_ref), channel_id=1, source_target_pairs={{2,4},{4,2},{3,5},{5,3},{10,12},{12,10},{11,13},{13,11},{18,20},{2... | collective-permute-start | bytes 811016 | tf_op jit(solution)/shard_map/ppermute | solution.py:336
  11.3 10.0 %collective-permute-start.3 = (f32[528,128]{1,0:T(8,128)S(1)}, f32[528,128]{1,0:T(8,128)S(1)}, u32[]{:S(2)}, u32[]{:S(2)}) collective-permute-start(f32[528,128]{1,0:T(8,128)S(1)} %collective-permute-done.swap_ref), channel_id=1, source_target_pairs={{0,2},{2,0},{4,6},{6,4},{1,3},{3,1},{5,7},{7,5},{8,10},{10,8},{12,... | collective-permute-start | bytes 811016 | tf_op jit(solution)/shard_map/ppermute | solution.py:335
  16.0 0.7 %copy-start.3 = (s32[32]{0:T(128)S(1)}, s32[32]{0:T(128)}, u32[]{:S(2)}) copy-start(s32[32]{0:T(128)} %slot_ref.1) | copy-start | bytes 388
  16.0 0.7 %copy-start.4 = (s32[32]{0:T(128)S(1)}, s32[32]{0:T(128)}, u32[]{:S(2)}) copy-start(s32[32]{0:T(128)} %day_ref.1) | copy-start | bytes 388
  21.9 6.6 %collective-permute-start.10 = (f32[4,32,128]{2,1,0:T(8,128)S(1)}, f32[4,32,128]{2,1,0:T(8,128)S(1)}, u32[]{:S(2)}, u32[]{:S(2)}) collective-permute-start(f32[4,32,128]{2,1,0:T(8,128)S(1)} %get-tuple-element.28), channel_id=1, source_target_pairs={{0,24},{1,25},{8,16},{9,17},{16,8},{17,9},{24,0},{25,1},{2,26},{3,... | collective-permute-start | bytes 196616 | tf_op jit(solution)/shard_map/ppermute | solution.py:345
  22.0 8.2 %collective-permute-start.11 = (f32[4,32,128]{2,1,0:T(8,128)S(1)}, f32[4,32,128]{2,1,0:T(8,128)S(1)}, u32[]{:S(2)}, u32[]{:S(2)}) collective-permute-start(f32[4,32,128]{2,1,0:T(8,128)S(1)} %get-tuple-element.29), channel_id=1, source_target_pairs={{0,25},{1,24},{8,17},{9,16},{16,9},{17,8},{24,1},{25,0},{2,27},{3,... | collective-permute-start | bytes 196616 | tf_op jit(solution)/shard_map/ppermute | solution.py:345
  25.2 5.5 %collective-permute-start.8 = (f32[4,32,128]{2,1,0:T(8,128)S(1)}, f32[4,32,128]{2,1,0:T(8,128)S(1)}, u32[]{:S(2)}, u32[]{:S(2)}) collective-permute-start(f32[4,32,128]{2,1,0:T(8,128)S(1)} %get-tuple-element.26), channel_id=1, source_target_pairs={{0,16},{1,17},{8,24},{9,25},{16,0},{17,1},{24,8},{25,9},{2,18},{3,... | collective-permute-start | bytes 196616 | tf_op jit(solution)/shard_map/ppermute | solution.py:345
  26.8 5.2 %collective-permute-start.9 = (f32[4,32,128]{2,1,0:T(8,128)S(1)}, f32[4,32,128]{2,1,0:T(8,128)S(1)}, u32[]{:S(2)}, u32[]{:S(2)}) collective-permute-start(f32[4,32,128]{2,1,0:T(8,128)S(1)} %get-tuple-element.27), channel_id=1, source_target_pairs={{0,17},{1,16},{8,25},{9,24},{16,1},{17,0},{24,9},{25,8},{2,19},{3,... | collective-permute-start | bytes 196616 | tf_op jit(solution)/shard_map/ppermute | solution.py:345
  27.9 4.1 %collective-permute-start.6 = (f32[4,32,128]{2,1,0:T(8,128)S(1)}, f32[4,32,128]{2,1,0:T(8,128)S(1)}, u32[]{:S(2)}, u32[]{:S(2)}) collective-permute-start(f32[4,32,128]{2,1,0:T(8,128)S(1)} %get-tuple-element.24), channel_id=1, source_target_pairs={{0,8},{1,9},{8,0},{9,1},{16,24},{17,25},{24,16},{25,17},{2,10},{3,... | collective-permute-start | bytes 196616 | tf_op jit(solution)/shard_map/ppermute | solution.py:345
  28.5 4.1 %collective-permute-start.7 = (f32[4,32,128]{2,1,0:T(8,128)S(1)}, f32[4,32,128]{2,1,0:T(8,128)S(1)}, u32[]{:S(2)}, u32[]{:S(2)}) collective-permute-start(f32[4,32,128]{2,1,0:T(8,128)S(1)} %get-tuple-element.25), channel_id=1, source_target_pairs={{0,9},{1,8},{8,1},{9,0},{16,25},{17,24},{24,17},{25,16},{2,11},{3,... | collective-permute-start | bytes 196616 | tf_op jit(solution)/shard_map/ppermute | solution.py:345
  30.2 4.3 %collective-permute-start.5 = (f32[4,32,128]{2,1,0:T(8,128)S(1)}, f32[4,32,128]{2,1,0:T(8,128)S(1)}, u32[]{:S(2)}, u32[]{:S(2)}) collective-permute-start(f32[4,32,128]{2,1,0:T(8,128)S(1)} %get-tuple-element.23), channel_id=1, source_target_pairs={{0,1},{1,0},{8,9},{9,8},{16,17},{17,16},{24,25},{25,24},{2,3},{3,2... | collective-permute-start | bytes 196616 | tf_op jit(solution)/shard_map/ppermute | solution.py:345

commit v2 on v1

--- a/solution.py
+++ b/solution.py
@@ -56,7 +56,7 @@
             jax.ShapeDtypeStruct((2, reactions, species), jnp.bfloat16),
             jax.ShapeDtypeStruct((species, reactions), jnp.bfloat16),
             jax.ShapeDtypeStruct((reactions, LANES), jnp.float32),
-            jax.ShapeDtypeStruct((span + rows,), jnp.int32),
+            jax.ShapeDtypeStruct((1, span + rows), jnp.int32),
         ),
         in_specs=[VMEM, VMEM, VMEM, SMEM, SMEM],
         out_specs=(VMEM, VMEM, VMEM, SMEM),
@@ -103,11 +103,11 @@
     note_slots(slot_ref, day_ref, band * span - reach, span + 2 * reach, band * span, source_of, lit_of)
     for half in range(PAIR):
         for slot, place in enumerate(places(lit_of, half * rows, rows)):
-            plan_ref[half * rows + place] = source_of[half * rows + slot]
+            plan_ref[0, half * rows + place] = source_of[half * rows + slot]
 
             @pl.when(side == half)
             def _():
-                plan_ref[span + place] = slot
+                plan_ref[0, span + place] = slot
 
 
 def flat_rows(field):
@@ -174,10 +174,9 @@
 
 def advect_kernel(
     turn, own_ref, swap_ref, own_a, own_b, swap_a, swap_b, plan_ref, same_ref, cross_ref,
-    window, flow, middle, advected, plan, sem,
+    window, flow, middle, advected,
 ):
-    fetch = pltpu.make_async_copy(plan_ref, plan, sem)
-    fetch.start()
+    plan = plan_ref[...]
     rows, species, width = same_ref.shape
     span = PAIR * rows
     reach = span // 2
@@ -221,10 +220,10 @@
 
     sweep(lambda row: window[row], courant, store_middle, start - 2, span + 2 * reach + 4)
     sweep(lambda row: middle[row], courant, store_advected, start, span + 2 * reach)
-    fetch.wait()
     for place in range(rows):
-        same_ref[place] = advected[plan[side * rows + place]]
-        cross_ref[place] = advected[plan[(1 - side) * rows + place]]
+        low, high = plan[0, place], plan[0, rows + place]
+        same_ref[place] = advected[jnp.where(side == 0, low, high)]
+        cross_ref[place] = advected[jnp.where(side == 0, high, low)]
 
 
 def advect(turn, fields, plan, parts, rows, columns):
@@ -242,8 +241,6 @@
             pltpu.VMEM((3 * span, 1, width), jnp.float32),
             pltpu.VMEM((3 * span, species, width), jnp.float32),
             pltpu.VMEM((2 * span, species, width), jnp.float32),
-            pltpu.SMEM(plan.shape, jnp.int32),
-            pltpu.SemaphoreType.DMA,
         ],
         compiler_params=params(8),
         cost_estimate=pl.CostEstimate(flops=4_000_000, bytes_accessed=400_000, transcendentals=0),
@@ -266,9 +263,8 @@
 
 def chemistry_kernel(count, *refs):
     chunks = refs[:count]
-    take_ref, net_ref, rate_ref, plan_ref, out_ref, cells, plan, sem = refs[count:]
-    fetch = pltpu.make_async_copy(plan_ref, plan, sem)
-    fetch.start()
+    take_ref, net_ref, rate_ref, plan_ref, out_ref, cells = refs[count:]
+    plan = plan_ref[...]
     rows, lines, width = chunks[0].shape
     species = count * lines
     lit_rows = rows // 2
@@ -288,8 +284,7 @@
         encounter = dot(twice(take_ref[0]), parts) * dot(twice(take_ref[1]), parts)
         rates = const * encounter / (1.0 + jnp.abs(encounter))
         conc = conc + dot(twice(net_ref[...]), split_rows(rates))
-    fetch.wait()
-    slot_of = [plan[PAIR * rows + place] for place in range(rows)]
+    slot_of = [plan[0, PAIR * rows + place] for place in range(rows)]
     for at, chunk in enumerate(chunks):
         source = lax.bitwise_xor(spec, at // PAIR) * PAIR + lax.bitwise_xor(side, at % PAIR)
         for place in range(lit_rows, rows):
@@ -306,11 +301,7 @@
         out_shape=jax.ShapeDtypeStruct((species * rows, width), jnp.float32),
         in_specs=[VMEM] * (len(chunks) + 4),
         out_specs=VMEM,
-        scratch_shapes=[
-            pltpu.VMEM((species, rows // 2 * width), jnp.float32),
-            pltpu.SMEM(plan.shape, jnp.int32),
-            pltpu.SemaphoreType.DMA,
-        ],
+        scratch_shapes=[pltpu.VMEM((species, rows // 2 * width), jnp.float32)],
         compiler_params=params(16),
         name="chemistry",
     )(*chunks, take, net, rates, plan)
@@ -330,10 +321,15 @@
     bands = lax.axis_size("band")
     own, other = pack(concentration, courant)
     swap = lax.ppermute(other, "pair", couples(PAIR, 0))
-    own_a = lax.ppermute(own, "band", couples(bands, 0))
-    own_b = lax.ppermute(own, "band", couples(bands, 1))
-    swap_a = lax.ppermute(swap, "band", couples(bands, 0))
-    swap_b = lax.ppermute(swap, "band", couples(bands, 1))
+
+    def exchange(block):
+        found = []
+        for first in (0, 1):
+            found.append(lax.ppermute(block, "band", couples(bands, first)))
+        return found
+
+    own_a, own_b = exchange(own)
+    swap_a, swap_b = exchange(swap)
     take, net, rates, plan = mechanism_tables(
         rate_const, reactants, products, block_slot, daylit, species_here * parts, rows
     )

time: 38 us -> 37.6 us (0.989)
  Pallas kernels: 8.9 us -> 8.47 us
    pallas_call x4, Pallas kernels: 2.25 us -> 1.86 us  [advect(): pl.pallas_call(functools.partial(advect_kernel, turn), out_shape=(chunk,...]
  transfers between devices with their start and end apart: 12 -> 12, of which waited for: 5 -> 6; matrix products, arithmetic and copies ran while one was open for 0% -> 0% of each run, Pallas kernels for 10% -> 10%
where the time goes in v2:
time: 37.6 us; the launch traced here: 37.4 us
  starting transfers between devices  20.6 us (55%)
  Pallas kernels  8.47 us (23%)
  waiting for transfers between devices  7.56 us (20%)
  local copies, waits for them, and re-layouts  0.67 us (2%)
    ppermute x4, starting transfers between devices, exchange(): found.append(lax.ppermute(block, 'band', couples(bands, first)))  10.5 us
    ppermute x7, starting transfers between devices, send(): chunks[at] = lax.ppermute(chunk, ('spec', 'pair'), pairs)  7.05 us
    ppermute x7, waiting for transfers between devices, send(): chunks[at] = lax.ppermute(chunk, ('spec', 'pair'), pairs)  3.73 us
    pallas_call x1, Pallas kernels, chemistry(): pl.pallas_call(functools.partial(chemistry_kernel, len(chunks)), out_shap...  3.32 us
    ppermute x1, starting transfers between devices, on_device(): swap = lax.ppermute(other, 'pair', couples(PAIR, 0))  3.03 us
    ppermute x4, waiting for transfers between devices, exchange(): found.append(lax.ppermute(block, 'band', couples(bands, first)))  2.47 us
    pallas_call x1, Pallas kernels, mechanism_tables(): pl.pallas_call(table_kernel, out_shape=(jax.ShapeDtypeStruct((2, reaction...  2.18 us
    pallas_call x4, Pallas kernels, advect(): pl.pallas_call(functools.partial(advect_kernel, turn), out_shape=(chunk,...  1.86 us
  transfers between devices with their start and end apart: 12, of which 6 were waited for; matrix products, arithmetic and copies ran while one was open for 0% of the time, Pallas kernels for 10%

profile of v2, /device:TPU:0, one launch (start us, length us, event | category | flops | bytes accessed | tf_op | source)
XLA Modules:
  0.0 37.4 jit_solution(13877330046648869795)
XLA Ops:
  0.0 0.0 copy-start.1
  0.0 0.0 copy-start.2
  0.0 1.1 %pack.1 = (f32[528,128]{1,0:T(8,128)S(1)}, f32[528,128]{1,0:T(8,128)S(1)}) custom-call(f32[1024,128]{1,0:T(8,128)} %bitcast.17, f32[16,128]{1,0:T(8,128)} %bitcast.18), custom_call_target="tpu_custom_call" | custom-call | tf_op jit(solution)/shard_map/pack/pallas_call | solution.py:139
  1.1 0.0 copy-start
  1.1 3.0 %collective-permute-start = (f32[528,128]{1,0:T(8,128)S(1)}, f32[528,128]{1,0:T(8,128)S(1)}, u32[]{:S(2)}, u32[]{:S(2)}) collective-permute-start(f32[528,128]{1,0:T(8,128)S(1)} %get-tuple-element.20), channel_id=1, source_target_pairs={{0,1},{1,0},{2,3},{3,2},{4,5},{5,4},{6,7},{7,6},{8,9},{9,8},{10,11... | collective-permute-start | bytes 811016 | tf_op jit(solution)/shard_map/ppermute | solution.py:323
  4.2 0.7 %collective-permute-start.2 = (f32[528,128]{1,0:T(8,128)S(1)}, f32[528,128]{1,0:T(8,128)S(1)}, u32[]{:S(2)}, u32[]{:S(2)}) collective-permute-start(f32[528,128]{1,0:T(8,128)S(1)} %get-tuple-element.19.own_ref), channel_id=1, source_target_pairs={{2,4},{4,2},{3,5},{5,3},{10,12},{12,10},{11,13},{13,11},{18,20},{2... | collective-permute-start | bytes 811016 | tf_op jit(solution)/shard_map/ppermute | solution.py:328
  4.8 4.4 %collective-permute-start.1 = (f32[528,128]{1,0:T(8,128)S(1)}, f32[528,128]{1,0:T(8,128)S(1)}, u32[]{:S(2)}, u32[]{:S(2)}) collective-permute-start(f32[528,128]{1,0:T(8,128)S(1)} %get-tuple-element.19.own_ref), channel_id=1, source_target_pairs={{0,2},{2,0},{4,6},{6,4},{1,3},{3,1},{5,7},{7,5},{8,10},{10,8},{12,... | collective-permute-start | bytes 811016 | tf_op jit(solution)/shard_map/ppermute | solution.py:328
  9.3 1.4 %collective-permute-done.swap_ref = f32[528,128]{1,0:T(8,128)S(1)} collective-permute-done((f32[528,128]{1,0:T(8,128)S(1)}, f32[528,128]{1,0:T(8,128)S(1)}, u32[]{:S(2)}, u32[]{:S(2)}) %collective-permute-start) | collective-permute-done | bytes 270368 | tf_op jit(solution)/shard_map/ppermute | solution.py:323
  10.6 0.7 %collective-permute-start.4 = (f32[528,128]{1,0:T(8,128)S(1)}, f32[528,128]{1,0:T(8,128)S(1)}, u32[]{:S(2)}, u32[]{:S(2)}) collective-permute-start(f32[528,128]{1,0:T(8,128)S(1)} %collective-permute-done.swap_ref), channel_id=1, source_target_pairs={{2,4},{4,2},{3,5},{5,3},{10,12},{12,10},{11,13},{13,11},{18,20},{2... | collective-permute-start | bytes 811016 | tf_op jit(solution)/shard_map/ppermute | solution.py:328
  11.3 4.7 %collective-permute-start.3 = (f32[528,128]{1,0:T(8,128)S(1)}, f32[528,128]{1,0:T(8,128)S(1)}, u32[]{:S(2)}, u32[]{:S(2)}) collective-permute-start(f32[528,128]{1,0:T(8,128)S(1)} %collective-permute-done.swap_ref), channel_id=1, source_target_pairs={{0,2},{2,0},{4,6},{6,4},{1,3},{3,1},{5,7},{7,5},{8,10},{10,8},{12,... | collective-permute-start | bytes 811016 | tf_op jit(solution)/shard_map/ppermute | solution.py:328
  16.0 0.0 copy-start.3
  16.0 0.0 copy-start.4
  16.0 0.0 copy-done.1
  16.0 0.0 copy-done.2
  16.0 0.0 copy-done
  16.0 0.6 %copy-done.3 = s32[32]{0:T(128)S(1)} copy-done((s32[32]{0:T(128)S(1)}, s32[32]{0:T(128)}, u32[]{:S(2)}) %copy-start.3) | copy-done | bytes 152
  16.7 0.0 copy-done.4
  16.7 2.2 %tables.1 = (bf16[2,1024,256]{2,1,0:T(8,128)(2,1)S(1)}, bf16[256,1024]{1,0:T(8,128)(2,1)S(1)}, f32[1024,128]{1,0:T(8,128)S(1)}, s32[1,12]{1,0:T(1,128)S(1)}) custom-call(s32[2,1024]{1,0:T(2,128)S(1)} %bitcast.14, s32[2,1024]{1,0:T(2,128)S(1)} %bitcast.15, f32[8,128]{1,0:T(8,128)S(1)} %bitcast.16, s32[32]{0:T(128)S(1)} %copy-done.3, s32[32]{0:T(128)S(1)} %copy-done.4), custom_call_target="tpu_custom_call" | custom-call | flops 20000000 | bytes 2000000 | tf_op jit(solution)/shard_map/tables/pallas_call | solution.py:53
  18.9 0.0 collective-permute-done.2.own_b
  18.9 0.0 collective-permute-done.1.own_a
  18.9 0.0 collective-permute-done.4.swap_b
  18.9 2.5 %collective-permute-done.3.swap_a = f32[528,128]{1,0:T(8,128)S(1)} collective-permute-done((f32[528,128]{1,0:T(8,128)S(1)}, f32[528,128]{1,0:T(8,128)S(1)}, u32[]{:S(2)}, u32[]{:S(2)}) %collective-permute-start.3) | collective-permute-done | bytes 270368 | tf_op jit(solution)/shard_map/ppermute | solution.py:328
  21.4 0.5 %shard_map.76 = (f32[4,32,128]{2,1,0:T(8,128)S(1)}, f32[4,32,128]{2,1,0:T(8,128)S(1)}) custom-call(f32[528,128]{1,0:T(8,128)S(1)} %get-tuple-element.19.own_ref, f32[528,128]{1,0:T(8,128)S(1)} %collective-permute-done.swap_ref, f32[528,128]{1,0:T(8,128)S(1)} %collective-permute-done.1.own_a, f32[528,128]{1,0:T(8,128)S(1)} %collective-permute-done.2.own_b, ...), custom_call_target="tpu_custom_call" | custom-call | flops 4000000 | bytes 400000 | tf_op jit(solution)/shard_map/pallas_call | solution.py:234
  21.8 0.1 collective-permute-start.10
  21.9 2.7 %collective-permute-start.11 = (f32[4,32,128]{2,1,0:T(8,128)S(1)}, f32[4,32,128]{2,1,0:T(8,128)S(1)}, u32[]{:S(2)}, u32[]{:S(2)}) collective-permute-start(f32[4,32,128]{2,1,0:T(8,128)S(1)} %get-tuple-element.29), channel_id=1, source_target_pairs={{0,25},{1,24},{8,17},{9,16},{16,9},{17,8},{24,1},{25,0},{2,27},{3,... | collective-permute-start | bytes 196616 | tf_op jit(solution)/shard_map/ppermute | solution.py:341
  24.6 0.5 %shard_map.75 = (f32[4,32,128]{2,1,0:T(8,128)S(1)}, f32[4,32,128]{2,1,0:T(8,128)S(1)}) custom-call(f32[528,128]{1,0:T(8,128)S(1)} %get-tuple-element.19.own_ref, f32[528,128]{1,0:T(8,128)S(1)} %collective-permute-done.swap_ref, f32[528,128]{1,0:T(8,128)S(1)} %collective-permute-done.1.own_a, f32[528,128]{1,0:T(8,128)S(1)} %collective-permute-done.2.own_b, ...), custom_call_target="tpu_custom_call" | custom-call | flops 4000000 | bytes 400000 | tf_op jit(solution)/shard_map/pallas_call | solution.py:234
  25.1 1.6 %collective-permute-start.8 = (f32[4,32,128]{2,1,0:T(8,128)S(1)}, f32[4,32,128]{2,1,0:T(8,128)S(1)}, u32[]{:S(2)}, u32[]{:S(2)}) collective-permute-start(f32[4,32,128]{2,1,0:T(8,128)S(1)} %get-tuple-element.26), channel_id=1, source_target_pairs={{0,16},{1,17},{8,24},{9,25},{16,0},{17,1},{24,8},{25,9},{2,18},{3,... | collective-permute-start | bytes 196616 | tf_op jit(solution)/shard_map/ppermute | solution.py:341
  26.6 0.5 %collective-permute-start.9 = (f32[4,32,128]{2,1,0:T(8,128)S(1)}, f32[4,32,128]{2,1,0:T(8,128)S(1)}, u32[]{:S(2)}, u32[]{:S(2)}) collective-permute-start(f32[4,32,128]{2,1,0:T(8,128)S(1)} %get-tuple-element.27), channel_id=1, source_target_pairs={{0,17},{1,16},{8,25},{9,24},{16,1},{17,0},{24,9},{25,8},{2,19},{3,... | collective-permute-start | bytes 196616 | tf_op jit(solution)/shard_map/ppermute | solution.py:341
  27.1 0.5 %shard_map.74 = (f32[4,32,128]{2,1,0:T(8,128)S(1)}, f32[4,32,128]{2,1,0:T(8,128)S(1)}) custom-call(f32[528,128]{1,0:T(8,128)S(1)} %get-tuple-element.19.own_ref, f32[528,128]{1,0:T(8,128)S(1)} %collective-permute-done.swap_ref, f32[528,128]{1,0:T(8,128)S(1)} %collective-permute-done.1.own_a, f32[528,128]{1,0:T(8,128)S(1)} %collective-permute-done.2.own_b, ...), custom_call_target="tpu_custom_call" | custom-call | flops 4000000 | bytes 400000 | tf_op jit(solution)/shard_map/pallas_call | solution.py:234
  27.6 0.1 collective-permute-start.6
  27.7 0.5 %shard_map.73 = (f32[4,32,128]{2,1,0:T(8,128)S(1)}, f32[4,32,128]{2,1,0:T(8,128)S(1)}) custom-call(f32[528,128]{1,0:T(8,128)S(1)} %get-tuple-element.19.own_ref, f32[528,128]{1,0:T(8,128)S(1)} %collective-permute-done.swap_ref, f32[528,128]{1,0:T(8,128)S(1)} %collective-permute-done.1.own_a, f32[528,128]{1,0:T(8,128)S(1)} %collective-permute-done.2.own_b, ...), custom_call_target="tpu_custom_call" | custom-call | flops 4000000 | bytes 400000 | tf_op jit(solution)/shard_map/pallas_call | solution.py:234
  28.1 0.0 collective-permute-done.10.refs_6_
  28.2 1.7 %collective-permute-start.7 = (f32[4,32,128]{2,1,0:T(8,128)S(1)}, f32[4,32,128]{2,1,0:T(8,128)S(1)}, u32[]{:S(2)}, u32[]{:S(2)}) collective-permute-start(f32[4,32,128]{2,1,0:T(8,128)S(1)} %get-tuple-element.25), channel_id=1, source_target_pairs={{0,9},{1,8},{8,1},{9,0},{16,25},{17,24},{24,17},{25,16},{2,11},{3,... | collective-permute-start | bytes 196616 | tf_op jit(solution)/shard_map/ppermute | solution.py:341
  29.8 0.0 collective-permute-done.11.refs_7_
  29.8 0.5 %collective-permute-start.5 = (f32[4,32,128]{2,1,0:T(8,128)S(1)}, f32[4,32,128]{2,1,0:T(8,128)S(1)}, u32[]{:S(2)}, u32[]{:S(2)}) collective-permute-start(f32[4,32,128]{2,1,0:T(8,128)S(1)} %get-tuple-element.23), channel_id=1, source_target_pairs={{0,1},{1,0},{8,9},{9,8},{16,17},{17,16},{24,25},{25,24},{2,3},{3,2... | collective-permute-start | bytes 196616 | tf_op jit(solution)/shard_map/ppermute | solution.py:341
  30.3 0.1 collective-permute-done.8.refs_4_
  30.4 1.4 %collective-permute-done.9.refs_5_ = f32[4,32,128]{2,1,0:T(8,128)S(1)} collective-permute-done((f32[4,32,128]{2,1,0:T(8,128)S(1)}, f32[4,32,128]{2,1,0:T(8,128)S(1)}, u32[]{:S(2)}, u32[]{:S(2)}) %collective-permute-start.9) | collective-permute-done | bytes 65568 | tf_op jit(solution)/shard_map/ppermute | solution.py:341
  31.8 0.0 collective-permute-done.6.refs_2_
  31.8 0.5 %collective-permute-done.7.refs_3_ = f32[4,32,128]{2,1,0:T(8,128)S(1)} collective-permute-done((f32[4,32,128]{2,1,0:T(8,128)S(1)}, f32[4,32,128]{2,1,0:T(8,128)S(1)}, u32[]{:S(2)}, u32[]{:S(2)}) %collective-permute-start.7) | collective-permute-done | bytes 65568 | tf_op jit(solution)/shard_map/ppermute | solution.py:341
  32.3 1.8 %collective-permute-done.5.refs_1_ = f32[4,32,128]{2,1,0:T(8,128)S(1)} collective-permute-done((f32[4,32,128]{2,1,0:T(8,128)S(1)}, f32[4,32,128]{2,1,0:T(8,128)S(1)}, u32[]{:S(2)}, u32[]{:S(2)}) %collective-permute-start.5) | collective-permute-done | bytes 65568 | tf_op jit(solution)/shard_map/ppermute | solution.py:341
  34.1 3.3 %chemistry.1 = f32[1024,128]{1,0:T(8,128)} custom-call(f32[4,32,128]{2,1,0:T(8,128)S(1)} %get-tuple-element.22.refs_0_, f32[4,32,128]{2,1,0:T(8,128)S(1)} %collective-permute-done.5.refs_1_, f32[4,32,128]{2,1,0:T(8,128)S(1)} %collective-permute-done.6.refs_2_, f32[4,32,128]{2,1,0:T(8,128)S(1)} %collective-permute-done.7.refs_3_, ...), custom_call_target="tpu_custom_call" | custom-call | tf_op jit(solution)/shard_map/chemistry/pallas_call | solution.py:299
Async XLA Ops:
  0.0 16.0 %copy-start.1 = (s32[1024,2]{0,1:T(2,128)S(1)}, s32[1024,2]{0,1:T(2,128)}, u32[]{:S(2)}) copy-start(s32[1024,2]{0,1:T(2,128)} %param.11) | copy-start | bytes 24580
  0.0 16.0 %copy-start.2 = (f32[1024]{0:T(1024)S(1)}, f32[1024]{0:T(1024)}, u32[]{:S(2)}) copy-start(f32[1024]{0:T(1024)} %param.9) | copy-start | bytes 12292
  1.1 14.9 %copy-start = (s32[1024,2]{0,1:T(2,128)S(1)}, s32[1024,2]{0,1:T(2,128)}, u32[]{:S(2)}) copy-start(s32[1024,2]{0,1:T(2,128)} %param.10) | copy-start | bytes 24580
  1.1 9.5 %collective-permute-start = (f32[528,128]{1,0:T(8,128)S(1)}, f32[528,128]{1,0:T(8,128)S(1)}, u32[]{:S(2)}, u32[]{:S(2)}) collective-permute-start(f32[528,128]{1,0:T(8,128)S(1)} %get-tuple-element.20), channel_id=1, source_target_pairs={{0,1},{1,0},{2,3},{3,2},{4,5},{5,4},{6,7},{7,6},{8,9},{9,8},{10,11... | collective-permute-start | bytes 811016 | tf_op jit(solution)/shard_map/ppermute | solution.py:323
  4.2 14.7 %collective-permute-start.2 = (f32[528,128]{1,0:T(8,128)S(1)}, f32[528,128]{1,0:T(8,128)S(1)}, u32[]{:S(2)}, u32[]{:S(2)}) collective-permute-start(f32[528,128]{1,0:T(8,128)S(1)} %get-tuple-element.19.own_ref), channel_id=1, source_target_pairs={{2,4},{4,2},{3,5},{5,3},{10,12},{12,10},{11,13},{13,11},{18,20},{2... | collective-permute-start | bytes 811016 | tf_op jit(solution)/shard_map/ppermute | solution.py:328
  4.8 14.1 %collective-permute-start.1 = (f32[528,128]{1,0:T(8,128)S(1)}, f32[528,128]{1,0:T(8,128)S(1)}, u32[]{:S(2)}, u32[]{:S(2)}) collective-permute-start(f32[528,128]{1,0:T(8,128)S(1)} %get-tuple-element.19.own_ref), channel_id=1, source_target_pairs={{0,2},{2,0},{4,6},{6,4},{1,3},{3,1},{5,7},{7,5},{8,10},{10,8},{12,... | collective-permute-start | bytes 811016 | tf_op jit(solution)/shard_map/ppermute | solution.py:328
  10.6 8.3 %collective-permute-start.4 = (f32[528,128]{1,0:T(8,128)S(1)}, f32[528,128]{1,0:T(8,128)S(1)}, u32[]{:S(2)}, u32[]{:S(2)}) collective-permute-start(f32[528,128]{1,0:T(8,128)S(1)} %collective-permute-done.swap_ref), channel_id=1, source_target_pairs={{2,4},{4,2},{3,5},{5,3},{10,12},{12,10},{11,13},{13,11},{18,20},{2... | collective-permute-start | bytes 811016 | tf_op jit(solution)/shard_map/ppermute | solution.py:328
  11.3 10.0 %collective-permute-start.3 = (f32[528,128]{1,0:T(8,128)S(1)}, f32[528,128]{1,0:T(8,128)S(1)}, u32[]{:S(2)}, u32[]{:S(2)}) collective-permute-start(f32[528,128]{1,0:T(8,128)S(1)} %collective-permute-done.swap_ref), channel_id=1, source_target_pairs={{0,2},{2,0},{4,6},{6,4},{1,3},{3,1},{5,7},{7,5},{8,10},{10,8},{12,... | collective-permute-start | bytes 811016 | tf_op jit(solution)/shard_map/ppermute | solution.py:328
  16.0 0.7 %copy-start.3 = (s32[32]{0:T(128)S(1)}, s32[32]{0:T(128)}, u32[]{:S(2)}) copy-start(s32[32]{0:T(128)} %slot_ref.1) | copy-start | bytes 388
  16.0 0.7 %copy-start.4 = (s32[32]{0:T(128)S(1)}, s32[32]{0:T(128)}, u32[]{:S(2)}) copy-start(s32[32]{0:T(128)} %day_ref.1) | copy-start | bytes 388
  21.8 6.3 %collective-permute-start.10 = (f32[4,32,128]{2,1,0:T(8,128)S(1)}, f32[4,32,128]{2,1,0:T(8,128)S(1)}, u32[]{:S(2)}, u32[]{:S(2)}) collective-permute-start(f32[4,32,128]{2,1,0:T(8,128)S(1)} %get-tuple-element.28), channel_id=1, source_target_pairs={{0,24},{1,25},{8,16},{9,17},{16,8},{17,9},{24,0},{25,1},{2,26},{3,... | collective-permute-start | bytes 196616 | tf_op jit(solution)/shard_map/ppermute | solution.py:341
  21.9 7.9 %collective-permute-start.11 = (f32[4,32,128]{2,1,0:T(8,128)S(1)}, f32[4,32,128]{2,1,0:T(8,128)S(1)}, u32[]{:S(2)}, u32[]{:S(2)}) collective-permute-start(f32[4,32,128]{2,1,0:T(8,128)S(1)} %get-tuple-element.29), channel_id=1, source_target_pairs={{0,25},{1,24},{8,17},{9,16},{16,9},{17,8},{24,1},{25,0},{2,27},{3,... | collective-permute-start | bytes 196616 | tf_op jit(solution)/shard_map/ppermute | solution.py:341
  25.1 5.4 %collective-permute-start.8 = (f32[4,32,128]{2,1,0:T(8,128)S(1)}, f32[4,32,128]{2,1,0:T(8,128)S(1)}, u32[]{:S(2)}, u32[]{:S(2)}) collective-permute-start(f32[4,32,128]{2,1,0:T(8,128)S(1)} %get-tuple-element.26), channel_id=1, source_target_pairs={{0,16},{1,17},{8,24},{9,25},{16,0},{17,1},{24,8},{25,9},{2,18},{3,... | collective-permute-start | bytes 196616 | tf_op jit(solution)/shard_map/ppermute | solution.py:341
  26.6 5.2 %collective-permute-start.9 = (f32[4,32,128]{2,1,0:T(8,128)S(1)}, f32[4,32,128]{2,1,0:T(8,128)S(1)}, u32[]{:S(2)}, u32[]{:S(2)}) collective-permute-start(f32[4,32,128]{2,1,0:T(8,128)S(1)} %get-tuple-element.27), channel_id=1, source_target_pairs={{0,17},{1,16},{8,25},{9,24},{16,1},{17,0},{24,9},{25,8},{2,19},{3,... | collective-permute-start | bytes 196616 | tf_op jit(solution)/shard_map/ppermute | solution.py:341
  27.6 4.2 %collective-permute-start.6 = (f32[4,32,128]{2,1,0:T(8,128)S(1)}, f32[4,32,128]{2,1,0:T(8,128)S(1)}, u32[]{:S(2)}, u32[]{:S(2)}) collective-permute-start(f32[4,32,128]{2,1,0:T(8,128)S(1)} %get-tuple-element.24), channel_id=1, source_target_pairs={{0,8},{1,9},{8,0},{9,1},{16,24},{17,25},{24,16},{25,17},{2,10},{3,... | collective-permute-start | bytes 196616 | tf_op jit(solution)/shard_map/ppermute | solution.py:341
  28.2 4.1 %collective-permute-start.7 = (f32[4,32,128]{2,1,0:T(8,128)S(1)}, f32[4,32,128]{2,1,0:T(8,128)S(1)}, u32[]{:S(2)}, u32[]{:S(2)}) collective-permute-start(f32[4,32,128]{2,1,0:T(8,128)S(1)} %get-tuple-element.25), channel_id=1, source_target_pairs={{0,9},{1,8},{8,1},{9,0},{16,25},{17,24},{24,17},{25,16},{2,11},{3,... | collective-permute-start | bytes 196616 | tf_op jit(solution)/shard_map/ppermute | solution.py:341
  29.8 4.3 %collective-permute-start.5 = (f32[4,32,128]{2,1,0:T(8,128)S(1)}, f32[4,32,128]{2,1,0:T(8,128)S(1)}, u32[]{:S(2)}, u32[]{:S(2)}) collective-permute-start(f32[4,32,128]{2,1,0:T(8,128)S(1)} %get-tuple-element.23), channel_id=1, source_target_pairs={{0,1},{1,0},{8,9},{9,8},{16,17},{17,16},{24,25},{25,24},{2,3},{3,2... | collective-permute-start | bytes 196616 | tf_op jit(solution)/shard_map/ppermute | solution.py:341

commit v3 on v2

--- a/solution.py
+++ b/solution.py
@@ -11,6 +11,7 @@
 
 SUBSTEPS = 2
 PAIR = 2
+CORES = 2
 LANES = 128
 VMEM = pl.BlockSpec(memory_space=pltpu.VMEM)
 SMEM = pl.BlockSpec(memory_space=pltpu.SMEM)
@@ -177,7 +178,7 @@
     window, flow, middle, advected,
 ):
     plan = plan_ref[...]
-    rows, species, width = same_ref.shape
+    cores, rows, species, width = same_ref.shape
     span = PAIR * rows
     reach = span // 2
     band = lax.axis_index("band")
@@ -186,51 +187,51 @@
     even = lax.rem(band, 2) == 0
     base_a = jnp.where(even, 2 * PAIR, 0)
     base_b = 2 * PAIR - base_a
-    part = lax.bitwise_xor(lax.axis_index("spec"), turn)
     pieces = width // LANES
     apart = own_ref.shape[0] // (species + 1)
-    for ref, place in (
-        (own_ref, PAIR + side),
-        (swap_ref, PAIR + 1 - side),
-        (own_a, base_a + side),
-        (own_b, base_b + side),
-        (swap_a, base_a + 1 - side),
-        (swap_b, base_b + 1 - side),
-    ):
-        for row in range(rows):
-            for piece in range(pieces):
-                at = (part * pieces + piece) * rows + row
-                lanes = slice(piece * LANES, (piece + 1) * LANES)
-                window[place * rows + row, :, lanes] = ref[pl.ds(at, species, stride=apart), :]
-                flow[place * rows + row, :, lanes] = ref[pl.ds(species * apart + at, 1), :]
-
     first_row = band * span - span
+    start = span - reach
 
     def courant(row):
         at = first_row + row
         return jnp.where((at >= 1) & (at <= total - 1), flow[row], 0.0)
 
-    start = span - reach
-
     def store_middle(row, value):
         middle[row] = value
 
     def store_advected(row, value):
         advected[row - start] = value
 
-    sweep(lambda row: window[row], courant, store_middle, start - 2, span + 2 * reach + 4)
-    sweep(lambda row: middle[row], courant, store_advected, start, span + 2 * reach)
-    for place in range(rows):
-        low, high = plan[0, place], plan[0, rows + place]
-        same_ref[place] = advected[jnp.where(side == 0, low, high)]
-        cross_ref[place] = advected[jnp.where(side == 0, high, low)]
+    for core in range(cores):
+        part = lax.bitwise_xor(lax.axis_index("spec"), turn * cores + core)
+        for ref, place in (
+            (own_ref, PAIR + side),
+            (swap_ref, PAIR + 1 - side),
+            (own_a, base_a + side),
+            (own_b, base_b + side),
+            (swap_a, base_a + 1 - side),
+            (swap_b, base_b + 1 - side),
+        ):
+            for row in range(rows):
+                for piece in range(pieces):
+                    at = (part * pieces + piece) * rows + row
+                    lanes = slice(piece * LANES, (piece + 1) * LANES)
+                    window[place * rows + row, :, lanes] = ref[pl.ds(at, species, stride=apart), :]
+                    flow[place * rows + row, :, lanes] = ref[pl.ds(species * apart + at, 1), :]
+
+        sweep(lambda row: window[row], courant, store_middle, start - 2, span + 2 * reach + 4)
+        sweep(lambda row: middle[row], courant, store_advected, start, span + 2 * reach)
+        for place in range(rows):
+            low, high = plan[0, place], plan[0, rows + place]
+            same_ref[core, place] = advected[jnp.where(side == 0, low, high)]
+            cross_ref[core, place] = advected[jnp.where(side == 0, high, low)]
 
 
 def advect(turn, fields, plan, parts, rows, columns):
     species = fields[0].shape[0] * LANES // (rows * columns) - 1
     span = PAIR * rows
     width = columns // parts
-    chunk = jax.ShapeDtypeStruct((rows, species, width), jnp.float32)
+    chunk = jax.ShapeDtypeStruct((CORES, rows, species, width), jnp.float32)
     return pl.pallas_call(
         functools.partial(advect_kernel, turn),
         out_shape=(chunk, chunk),
@@ -265,7 +266,7 @@
     chunks = refs[:count]
     take_ref, net_ref, rate_ref, plan_ref, out_ref, cells = refs[count:]
     plan = plan_ref[...]
-    rows, lines, width = chunks[0].shape
+    rows, lines, width = chunks[0].shape[1:]
     species = count * lines
     lit_rows = rows // 2
     copies = lit_rows * width // LANES
@@ -275,7 +276,7 @@
         source = lax.bitwise_xor(spec, at // PAIR) * PAIR + lax.bitwise_xor(side, at % PAIR)
         first = pl.multiple_of(source * lines, lines)
         for place in range(lit_rows):
-            cells[pl.ds(first, lines), place * width : (place + 1) * width] = chunk[place]
+            cells[pl.ds(first, lines), place * width : (place + 1) * width] = chunk[at // PAIR % CORES, place]
 
     conc = cells[...]
     const = jnp.concatenate([rate_ref[...]] * copies, axis=1)
@@ -288,13 +289,13 @@
     for at, chunk in enumerate(chunks):
         source = lax.bitwise_xor(spec, at // PAIR) * PAIR + lax.bitwise_xor(side, at % PAIR)
         for place in range(lit_rows, rows):
-            out_ref[pl.ds(source * (lines * rows) + slot_of[place], lines, stride=rows), :] = chunk[place]
+            out_ref[pl.ds(source * (lines * rows) + slot_of[place], lines, stride=rows), :] = chunk[at // PAIR % CORES, place]
     for place in range(lit_rows):
         out_ref[pl.ds(slot_of[place], species, stride=rows), :] = conc[:, place * width : (place + 1) * width]
 
 
 def chemistry(chunks, take, net, rates, plan):
-    rows, lines, width = chunks[0].shape
+    rows, lines, width = chunks[0].shape[1:]
     species = len(chunks) * lines
     flat = pl.pallas_call(
         functools.partial(chemistry_kernel, len(chunks)),
@@ -336,16 +337,19 @@
     fields = (own, swap, own_a, own_b, swap_a, swap_b)
     chunks = [None] * (parts * PAIR)
 
-    def send(chunk, at):
-        pairs = [(peer, peer ^ at) for peer in range(parts * PAIR)]
-        chunks[at] = lax.ppermute(chunk, ("spec", "pair"), pairs)
-
-    for turn in reversed(range(parts)):
-        same, cross = advect(turn, fields, plan, parts, rows, columns)
-        send(cross, turn * PAIR + 1)
-        if turn:
-            send(same, turn * PAIR)
-    chunks[0] = same
+    def send(chunk, step):
+        pairs = [(peer, peer ^ step) for peer in range(parts * PAIR)]
+        return lax.ppermute(chunk, ("spec", "pair"), pairs)
+
+    for turn in reversed(range(parts // CORES)):
+        blocks = advect(turn, fields, plan, parts, rows, columns)
+        for side in range(PAIR):
+            at = turn * CORES * PAIR + side
+            chunks[at] = send(blocks[side], at) if at else blocks[side]
+    for turn in range(parts // CORES):
+        for side in range(PAIR):
+            at = turn * CORES * PAIR + side
+            chunks[at + PAIR] = send(chunks[at], PAIR)
     return chemistry(chunks, take, net, rates, plan)
 
 

time: 37.6 us -> 36 us (0.957)
  starting transfers between devices: 20.6 us -> 17.1 us
  waiting for transfers between devices: 7.56 us -> 9.59 us
    ppermute x7, starting transfers between devices: 7.05 us -> 3.63 us  [send(): return lax.ppermute(chunk, ('spec', 'pair'), pairs)]
    ppermute x7, waiting for transfers between devices: 3.73 us -> 5.76 us  [send(): return lax.ppermute(chunk, ('spec', 'pair'), pairs)]
    pallas_call x4 -> x2, Pallas kernels: 1.86 us -> 1.75 us  [advect(): pl.pallas_call(functools.partial(advect_kernel, turn), out_shape=(chunk,...]
  transfers between devices with their start and end apart: 12 -> 12, of which waited for: 6 -> 7; matrix products, arithmetic and copies ran while one was open for 0% -> 0% of each run, Pallas kernels for 10% -> 9%
where the time goes in v3:
time: 36 us; the launch traced here: 35.8 us
  starting transfers between devices  17.1 us (48%)
  waiting for transfers between devices  9.59 us (27%)
  Pallas kernels  8.34 us (23%)
  local copies, waits for them, and re-layouts  0.67 us (2%)
    ppermute x4, starting transfers between devices, exchange(): found.append(lax.ppermute(block, 'band', couples(bands, first)))  10.5 us
    ppermute x7, waiting for transfers between devices, send(): return lax.ppermute(chunk, ('spec', 'pair'), pairs)  5.76 us
    ppermute x7, starting transfers between devices, send(): return lax.ppermute(chunk, ('spec', 'pair'), pairs)  3.63 us
    pallas_call x1, Pallas kernels, chemistry(): pl.pallas_call(functools.partial(chemistry_kernel, len(chunks)), out_shap...  3.31 us
    ppermute x1, starting transfers between devices, on_device(): swap = lax.ppermute(other, 'pair', couples(PAIR, 0))  3.03 us
    ppermute x4, waiting for transfers between devices, exchange(): found.append(lax.ppermute(block, 'band', couples(bands, first)))  2.47 us
    pallas_call x1, Pallas kernels, mechanism_tables(): pl.pallas_call(table_kernel, out_shape=(jax.ShapeDtypeStruct((2, reaction...  2.18 us
    pallas_call x2, Pallas kernels, advect(): pl.pallas_call(functools.partial(advect_kernel, turn), out_shape=(chunk,...  1.75 us
  transfers between devices with their start and end apart: 12, of which 7 were waited for; matrix products, arithmetic and copies ran while one was open for 0% of the time, Pallas kernels for 9%

profile of v3, /device:TPU:0, one launch (start us, length us, event | category | flops | bytes accessed | tf_op | source)
XLA Modules:
  0.0 35.8 jit_solution(6111317229884127804)
XLA Ops:
  0.0 0.0 copy-start.1
  0.0 0.0 copy-start.2
  0.0 1.1 %pack.1 = (f32[528,128]{1,0:T(8,128)S(1)}, f32[528,128]{1,0:T(8,128)S(1)}) custom-call(f32[1024,128]{1,0:T(8,128)} %bitcast.17, f32[16,128]{1,0:T(8,128)} %bitcast.18), custom_call_target="tpu_custom_call" | custom-call | tf_op jit(solution)/shard_map/pack/pallas_call | solution.py:140
  1.1 0.0 copy-start
  1.1 3.0 %collective-permute-start = (f32[528,128]{1,0:T(8,128)S(1)}, f32[528,128]{1,0:T(8,128)S(1)}, u32[]{:S(2)}, u32[]{:S(2)}) collective-permute-start(f32[528,128]{1,0:T(8,128)S(1)} %get-tuple-element.16), channel_id=1, source_target_pairs={{0,1},{1,0},{2,3},{3,2},{4,5},{5,4},{6,7},{7,6},{8,9},{9,8},{10,11... | collective-permute-start | bytes 811016 | tf_op jit(solution)/shard_map/ppermute | solution.py:324
  4.2 0.7 %collective-permute-start.2 = (f32[528,128]{1,0:T(8,128)S(1)}, f32[528,128]{1,0:T(8,128)S(1)}, u32[]{:S(2)}, u32[]{:S(2)}) collective-permute-start(f32[528,128]{1,0:T(8,128)S(1)} %get-tuple-element.15.own_ref), channel_id=1, source_target_pairs={{2,4},{4,2},{3,5},{5,3},{10,12},{12,10},{11,13},{13,11},{18,20},{2... | collective-permute-start | bytes 811016 | tf_op jit(solution)/shard_map/ppermute | solution.py:329
  4.8 4.4 %collective-permute-start.1 = (f32[528,128]{1,0:T(8,128)S(1)}, f32[528,128]{1,0:T(8,128)S(1)}, u32[]{:S(2)}, u32[]{:S(2)}) collective-permute-start(f32[528,128]{1,0:T(8,128)S(1)} %get-tuple-element.15.own_ref), channel_id=1, source_target_pairs={{0,2},{2,0},{4,6},{6,4},{1,3},{3,1},{5,7},{7,5},{8,10},{10,8},{12,... | collective-permute-start | bytes 811016 | tf_op jit(solution)/shard_map/ppermute | solution.py:329
  9.3 1.4 %collective-permute-done.swap_ref = f32[528,128]{1,0:T(8,128)S(1)} collective-permute-done((f32[528,128]{1,0:T(8,128)S(1)}, f32[528,128]{1,0:T(8,128)S(1)}, u32[]{:S(2)}, u32[]{:S(2)}) %collective-permute-start) | collective-permute-done | bytes 270368 | tf_op jit(solution)/shard_map/ppermute | solution.py:324
  10.6 0.7 %collective-permute-start.4 = (f32[528,128]{1,0:T(8,128)S(1)}, f32[528,128]{1,0:T(8,128)S(1)}, u32[]{:S(2)}, u32[]{:S(2)}) collective-permute-start(f32[528,128]{1,0:T(8,128)S(1)} %collective-permute-done.swap_ref), channel_id=1, source_target_pairs={{2,4},{4,2},{3,5},{5,3},{10,12},{12,10},{11,13},{13,11},{18,20},{2... | collective-permute-start | bytes 811016 | tf_op jit(solution)/shard_map/ppermute | solution.py:329
  11.3 4.7 %collective-permute-start.3 = (f32[528,128]{1,0:T(8,128)S(1)}, f32[528,128]{1,0:T(8,128)S(1)}, u32[]{:S(2)}, u32[]{:S(2)}) collective-permute-start(f32[528,128]{1,0:T(8,128)S(1)} %collective-permute-done.swap_ref), channel_id=1, source_target_pairs={{0,2},{2,0},{4,6},{6,4},{1,3},{3,1},{5,7},{7,5},{8,10},{10,8},{12,... | collective-permute-start | bytes 811016 | tf_op jit(solution)/shard_map/ppermute | solution.py:329
  16.0 0.0 copy-start.3
  16.0 0.0 copy-start.4
  16.0 0.0 copy-done.1
  16.0 0.0 copy-done.2
  16.0 0.0 copy-done
  16.0 0.6 %copy-done.3 = s32[32]{0:T(128)S(1)} copy-done((s32[32]{0:T(128)S(1)}, s32[32]{0:T(128)}, u32[]{:S(2)}) %copy-start.3) | copy-done | bytes 152
  16.7 0.0 copy-done.4
  16.7 2.2 %tables.1 = (bf16[2,1024,256]{2,1,0:T(8,128)(2,1)S(1)}, bf16[256,1024]{1,0:T(8,128)(2,1)S(1)}, f32[1024,128]{1,0:T(8,128)S(1)}, s32[1,12]{1,0:T(1,128)S(1)}) custom-call(s32[2,1024]{1,0:T(2,128)S(1)} %bitcast.14, s32[2,1024]{1,0:T(2,128)S(1)} %bitcast.15, f32[8,128]{1,0:T(8,128)S(1)} %bitcast.16, s32[32]{0:T(128)S(1)} %copy-done.3, s32[32]{0:T(128)S(1)} %copy-done.4), custom_call_target="tpu_custom_call" | custom-call | flops 20000000 | bytes 2000000 | tf_op jit(solution)/shard_map/tables/pallas_call | solution.py:54
  18.9 0.0 collective-permute-done.2.own_b
  18.9 0.0 collective-permute-done.1.own_a
  18.9 0.0 collective-permute-done.4.swap_b
  18.9 2.5 %collective-permute-done.3.swap_a = f32[528,128]{1,0:T(8,128)S(1)} collective-permute-done((f32[528,128]{1,0:T(8,128)S(1)}, f32[528,128]{1,0:T(8,128)S(1)}, u32[]{:S(2)}, u32[]{:S(2)}) %collective-permute-start.3) | collective-permute-done | bytes 270368 | tf_op jit(solution)/shard_map/ppermute | solution.py:329
  21.4 0.9 %shard_map.74 = (f32[2,4,32,128]{3,2,1,0:T(8,128)S(1)}, f32[2,4,32,128]{3,2,1,0:T(8,128)S(1)}) custom-call(f32[528,128]{1,0:T(8,128)S(1)} %get-tuple-element.15.own_ref, f32[528,128]{1,0:T(8,128)S(1)} %collective-permute-done.swap_ref, f32[528,128]{1,0:T(8,128)S(1)} %collective-permute-done.1.own_a, f32[528,128]{1,0:T(8,128)S(1)} %collective-permute-done.2.own_b, ...), custom_call_target="tpu_custom_call" | custom-call | flops 4000000 | bytes 400000 | tf_op jit(solution)/shard_map/pallas_call | solution.py:235
  22.2 1.6 %collective-permute-start.8 = (f32[2,4,32,128]{3,2,1,0:T(8,128)S(1)}, f32[2,4,32,128]{3,2,1,0:T(8,128)S(1)}, u32[]{:S(2)}, u32[]{:S(2)}) collective-permute-start(f32[2,4,32,128]{3,2,1,0:T(8,128)S(1)} %get-tuple-element.20), channel_id=1, source_target_pairs={{0,16},{1,17},{8,24},{9,25},{16,0},{17,1},{24,8},{25,9},{2,18},{3,... | collective-permute-start | bytes 393224 | tf_op jit(solution)/shard_map/ppermute | solution.py:342
  23.8 1.4 %collective-permute-start.9 = (f32[2,4,32,128]{3,2,1,0:T(8,128)S(1)}, f32[2,4,32,128]{3,2,1,0:T(8,128)S(1)}, u32[]{:S(2)}, u32[]{:S(2)}) collective-permute-start(f32[2,4,32,128]{3,2,1,0:T(8,128)S(1)} %get-tuple-element.21), channel_id=1, source_target_pairs={{0,17},{1,16},{8,25},{9,24},{16,1},{17,0},{24,9},{25,8},{2,19},{3,... | collective-permute-start | bytes 393224 | tf_op jit(solution)/shard_map/ppermute | solution.py:342
  25.3 0.9 %shard_map.73 = (f32[2,4,32,128]{3,2,1,0:T(8,128)S(1)}, f32[2,4,32,128]{3,2,1,0:T(8,128)S(1)}) custom-call(f32[528,128]{1,0:T(8,128)S(1)} %get-tuple-element.15.own_ref, f32[528,128]{1,0:T(8,128)S(1)} %collective-permute-done.swap_ref, f32[528,128]{1,0:T(8,128)S(1)} %collective-permute-done.1.own_a, f32[528,128]{1,0:T(8,128)S(1)} %collective-permute-done.2.own_b, ...), custom_call_target="tpu_custom_call" | custom-call | flops 4000000 | bytes 400000 | tf_op jit(solution)/shard_map/pallas_call | solution.py:235
  26.1 0.6 %collective-permute-start.5 = (f32[2,4,32,128]{3,2,1,0:T(8,128)S(1)}, f32[2,4,32,128]{3,2,1,0:T(8,128)S(1)}, u32[]{:S(2)}, u32[]{:S(2)}) collective-permute-start(f32[2,4,32,128]{3,2,1,0:T(8,128)S(1)} %get-tuple-element.19), channel_id=1, source_target_pairs={{0,1},{1,0},{8,9},{9,8},{16,17},{17,16},{24,25},{25,24},{2,3},{3,2... | collective-permute-start | bytes 393224 | tf_op jit(solution)/shard_map/ppermute | solution.py:342
  26.7 0.0 collective-permute-start.6
  26.8 1.2 %collective-permute-done.8.refs_4_ = f32[2,4,32,128]{3,2,1,0:T(8,128)S(1)} collective-permute-done((f32[2,4,32,128]{3,2,1,0:T(8,128)S(1)}, f32[2,4,32,128]{3,2,1,0:T(8,128)S(1)}, u32[]{:S(2)}, u32[]{:S(2)}) %collective-permute-start.8) | collective-permute-done | bytes 131104 | tf_op jit(solution)/shard_map/ppermute | solution.py:342
  28.0 0.0 collective-permute-start.10
  28.0 2.1 %collective-permute-done.9.refs_5_ = f32[2,4,32,128]{3,2,1,0:T(8,128)S(1)} collective-permute-done((f32[2,4,32,128]{3,2,1,0:T(8,128)S(1)}, f32[2,4,32,128]{3,2,1,0:T(8,128)S(1)}, u32[]{:S(2)}, u32[]{:S(2)}) %collective-permute-start.9) | collective-permute-done | bytes 131104 | tf_op jit(solution)/shard_map/ppermute | solution.py:342
  30.1 0.0 collective-permute-start.11
  30.1 1.0 %collective-permute-done.5.refs_1_ = f32[2,4,32,128]{3,2,1,0:T(8,128)S(1)} collective-permute-done((f32[2,4,32,128]{3,2,1,0:T(8,128)S(1)}, f32[2,4,32,128]{3,2,1,0:T(8,128)S(1)}, u32[]{:S(2)}, u32[]{:S(2)}) %collective-permute-start.5) | collective-permute-done | bytes 131104 | tf_op jit(solution)/shard_map/ppermute | solution.py:342
  31.2 0.0 collective-permute-start.7
  31.2 0.0 collective-permute-done.6.refs_2_
  31.2 0.0 collective-permute-done.10.refs_6_
  31.2 0.3 collective-permute-done.11.refs_7_
  31.5 1.0 %collective-permute-done.7.refs_3_ = f32[2,4,32,128]{3,2,1,0:T(8,128)S(1)} collective-permute-done((f32[2,4,32,128]{3,2,1,0:T(8,128)S(1)}, f32[2,4,32,128]{3,2,1,0:T(8,128)S(1)}, u32[]{:S(2)}, u32[]{:S(2)}) %collective-permute-start.7) | collective-permute-done | bytes 131104 | tf_op jit(solution)/shard_map/ppermute | solution.py:342
  32.5 3.3 %chemistry.1 = f32[1024,128]{1,0:T(8,128)} custom-call(f32[2,4,32,128]{3,2,1,0:T(8,128)S(1)} %get-tuple-element.18.refs_0_, f32[2,4,32,128]{3,2,1,0:T(8,128)S(1)} %collective-permute-done.5.refs_1_, f32[2,4,32,128]{3,2,1,0:T(8,128)S(1)} %collective-permute-done.6.refs_2_, f32[2,4,32,128]{3,2,1,0:T(8,128)S(1)} %collective-permute-done.7.refs_3_, ...), custom_call_target="tpu_custom_call" | custom-call | tf_op jit(solution)/shard_map/chemistry/pallas_call | solution.py:300
Async XLA Ops:
  0.0 16.0 %copy-start.1 = (s32[1024,2]{0,1:T(2,128)S(1)}, s32[1024,2]{0,1:T(2,128)}, u32[]{:S(2)}) copy-start(s32[1024,2]{0,1:T(2,128)} %param.11) | copy-start | bytes 24580
  0.0 16.0 %copy-start.2 = (f32[1024]{0:T(1024)S(1)}, f32[1024]{0:T(1024)}, u32[]{:S(2)}) copy-start(f32[1024]{0:T(1024)} %param.9) | copy-start | bytes 12292
  1.1 14.9 %copy-start = (s32[1024,2]{0,1:T(2,128)S(1)}, s32[1024,2]{0,1:T(2,128)}, u32[]{:S(2)}) copy-start(s32[1024,2]{0,1:T(2,128)} %param.10) | copy-start | bytes 24580
  1.1 9.5 %collective-permute-start = (f32[528,128]{1,0:T(8,128)S(1)}, f32[528,128]{1,0:T(8,128)S(1)}, u32[]{:S(2)}, u32[]{:S(2)}) collective-permute-start(f32[528,128]{1,0:T(8,128)S(1)} %get-tuple-element.16), channel_id=1, source_target_pairs={{0,1},{1,0},{2,3},{3,2},{4,5},{5,4},{6,7},{7,6},{8,9},{9,8},{10,11... | collective-permute-start | bytes 811016 | tf_op jit(solution)/shard_map/ppermute | solution.py:324
  4.2 14.7 %collective-permute-start.2 = (f32[528,128]{1,0:T(8,128)S(1)}, f32[528,128]{1,0:T(8,128)S(1)}, u32[]{:S(2)}, u32[]{:S(2)}) collective-permute-start(f32[528,128]{1,0:T(8,128)S(1)} %get-tuple-element.15.own_ref), channel_id=1, source_target_pairs={{2,4},{4,2},{3,5},{5,3},{10,12},{12,10},{11,13},{13,11},{18,20},{2... | collective-permute-start | bytes 811016 | tf_op jit(solution)/shard_map/ppermute | solution.py:329
  4.8 14.1 %collective-permute-start.1 = (f32[528,128]{1,0:T(8,128)S(1)}, f32[528,128]{1,0:T(8,128)S(1)}, u32[]{:S(2)}, u32[]{:S(2)}) collective-permute-start(f32[528,128]{1,0:T(8,128)S(1)} %get-tuple-element.15.own_ref), channel_id=1, source_target_pairs={{0,2},{2,0},{4,6},{6,4},{1,3},{3,1},{5,7},{7,5},{8,10},{10,8},{12,... | collective-permute-start | bytes 811016 | tf_op jit(solution)/shard_map/ppermute | solution.py:329
  10.6 8.3 %collective-permute-start.4 = (f32[528,128]{1,0:T(8,128)S(1)}, f32[528,128]{1,0:T(8,128)S(1)}, u32[]{:S(2)}, u32[]{:S(2)}) collective-permute-start(f32[528,128]{1,0:T(8,128)S(1)} %collective-permute-done.swap_ref), channel_id=1, source_target_pairs={{2,4},{4,2},{3,5},{5,3},{10,12},{12,10},{11,13},{13,11},{18,20},{2... | collective-permute-start | bytes 811016 | tf_op jit(solution)/shard_map/ppermute | solution.py:329
  11.3 10.0 %collective-permute-start.3 = (f32[528,128]{1,0:T(8,128)S(1)}, f32[528,128]{1,0:T(8,128)S(1)}, u32[]{:S(2)}, u32[]{:S(2)}) collective-permute-start(f32[528,128]{1,0:T(8,128)S(1)} %collective-permute-done.swap_ref), channel_id=1, source_target_pairs={{0,2},{2,0},{4,6},{6,4},{1,3},{3,1},{5,7},{7,5},{8,10},{10,8},{12,... | collective-permute-start | bytes 811016 | tf_op jit(solution)/shard_map/ppermute | solution.py:329
  16.0 0.7 %copy-start.3 = (s32[32]{0:T(128)S(1)}, s32[32]{0:T(128)}, u32[]{:S(2)}) copy-start(s32[32]{0:T(128)} %slot_ref.1) | copy-start | bytes 388
  16.0 0.7 %copy-start.4 = (s32[32]{0:T(128)S(1)}, s32[32]{0:T(128)}, u32[]{:S(2)}) copy-start(s32[32]{0:T(128)} %day_ref.1) | copy-start | bytes 388
  22.2 5.7 %collective-permute-start.8 = (f32[2,4,32,128]{3,2,1,0:T(8,128)S(1)}, f32[2,4,32,128]{3,2,1,0:T(8,128)S(1)}, u32[]{:S(2)}, u32[]{:S(2)}) collective-permute-start(f32[2,4,32,128]{3,2,1,0:T(8,128)S(1)} %get-tuple-element.20), channel_id=1, source_target_pairs={{0,16},{1,17},{8,24},{9,25},{16,0},{17,1},{24,8},{25,9},{2,18},{3,... | collective-permute-start | bytes 393224 | tf_op jit(solution)/shard_map/ppermute | solution.py:342
  23.8 6.3 %collective-permute-start.9 = (f32[2,4,32,128]{3,2,1,0:T(8,128)S(1)}, f32[2,4,32,128]{3,2,1,0:T(8,128)S(1)}, u32[]{:S(2)}, u32[]{:S(2)}) collective-permute-start(f32[2,4,32,128]{3,2,1,0:T(8,128)S(1)} %get-tuple-element.21), channel_id=1, source_target_pairs={{0,17},{1,16},{8,25},{9,24},{16,1},{17,0},{24,9},{25,8},{2,19},{3,... | collective-permute-start | bytes 393224 | tf_op jit(solution)/shard_map/ppermute | solution.py:342
  26.1 5.0 %collective-permute-start.5 = (f32[2,4,32,128]{3,2,1,0:T(8,128)S(1)}, f32[2,4,32,128]{3,2,1,0:T(8,128)S(1)}, u32[]{:S(2)}, u32[]{:S(2)}) collective-permute-start(f32[2,4,32,128]{3,2,1,0:T(8,128)S(1)} %get-tuple-element.19), channel_id=1, source_target_pairs={{0,1},{1,0},{8,9},{9,8},{16,17},{17,16},{24,25},{25,24},{2,3},{3,2... | collective-permute-start | bytes 393224 | tf_op jit(solution)/shard_map/ppermute | solution.py:342
  26.7 4.4 %collective-permute-start.6 = (f32[2,4,32,128]{3,2,1,0:T(8,128)S(1)}, f32[2,4,32,128]{3,2,1,0:T(8,128)S(1)}, u32[]{:S(2)}, u32[]{:S(2)}) collective-permute-start(f32[2,4,32,128]{3,2,1,0:T(8,128)S(1)} %get-tuple-element.18.refs_0_), channel_id=1, source_target_pairs={{0,8},{1,9},{8,0},{9,1},{16,24},{17,25},{24,16},{25,17},{2,10},{3,... | collective-permute-start | bytes 393224 | tf_op jit(solution)/shard_map/ppermute | solution.py:342
  28.0 3.2 %collective-permute-start.10 = (f32[2,4,32,128]{3,2,1,0:T(8,128)S(1)}, f32[2,4,32,128]{3,2,1,0:T(8,128)S(1)}, u32[]{:S(2)}, u32[]{:S(2)}) collective-permute-start(f32[2,4,32,128]{3,2,1,0:T(8,128)S(1)} %collective-permute-done.8.refs_4_), channel_id=1, source_target_pairs={{0,8},{1,9},{8,0},{9,1},{16,24},{17,25},{24,16},{25,17},{2,10},{3,... | collective-permute-start | bytes 393224 | tf_op jit(solution)/shard_map/ppermute | solution.py:342
  30.1 1.3 %collective-permute-start.11 = (f32[2,4,32,128]{3,2,1,0:T(8,128)S(1)}, f32[2,4,32,128]{3,2,1,0:T(8,128)S(1)}, u32[]{:S(2)}, u32[]{:S(2)}) collective-permute-start(f32[2,4,32,128]{3,2,1,0:T(8,128)S(1)} %collective-permute-done.9.refs_5_), channel_id=1, source_target_pairs={{0,8},{1,9},{8,0},{9,1},{16,24},{17,25},{24,16},{25,17},{2,10},{3,... | collective-permute-start | bytes 393224 | tf_op jit(solution)/shard_map/ppermute | solution.py:342
  31.2 1.3 %collective-permute-start.7 = (f32[2,4,32,128]{3,2,1,0:T(8,128)S(1)}, f32[2,4,32,128]{3,2,1,0:T(8,128)S(1)}, u32[]{:S(2)}, u32[]{:S(2)}) collective-permute-start(f32[2,4,32,128]{3,2,1,0:T(8,128)S(1)} %collective-permute-done.5.refs_1_), channel_id=1, source_target_pairs={{0,8},{1,9},{8,0},{9,1},{16,24},{17,25},{24,16},{25,17},{2,10},{3,... | collective-permute-start | bytes 393224 | tf_op jit(solution)/shard_map/ppermute | solution.py:342

commit v4 on v3

--- a/solution.py
+++ b/solution.py
@@ -57,7 +57,7 @@
             jax.ShapeDtypeStruct((2, reactions, species), jnp.bfloat16),
             jax.ShapeDtypeStruct((species, reactions), jnp.bfloat16),
             jax.ShapeDtypeStruct((reactions, LANES), jnp.float32),
-            jax.ShapeDtypeStruct((1, span + rows), jnp.int32),
+            jax.ShapeDtypeStruct((1, span + 3 * rows + 2), jnp.int32),
         ),
         in_specs=[VMEM, VMEM, VMEM, SMEM, SMEM],
         out_specs=(VMEM, VMEM, VMEM, SMEM),
@@ -102,13 +102,35 @@
     side = lax.axis_index("pair")
     reach = span // 2
     note_slots(slot_ref, day_ref, band * span - reach, span + 2 * reach, band * span, source_of, lit_of)
+    codes, early, late = span + rows, span + 2 * rows, span + 3 * rows
+    for at in range(early, late + 2):
+        plan_ref[0, at] = 0
     for half in range(PAIR):
-        for slot, place in enumerate(places(lit_of, half * rows, rows)):
-            plan_ref[0, half * rows + place] = source_of[half * rows + slot]
+        found = places(lit_of, half * rows, rows)
+        first = reach + half * rows
+        rank = jnp.int32(0)
+        for slot, place in enumerate(found):
+            source = source_of[half * rows + slot]
+            plan_ref[0, half * rows + place] = source
+            stays = (source >= first) & (source < first + rows)
+            moves = (source >= reach) & (source < reach + span)
+            kept = jnp.minimum(rank, rows - 2)
+            code = jnp.where(stays, kept, jnp.where(moves, rows - 1, rows))
 
             @pl.when(side == half)
             def _():
                 plan_ref[0, span + place] = slot
+                plan_ref[0, codes + place] = code
+
+            @pl.when((side != half) & stays)
+            def _():
+                plan_ref[0, early + kept] = source - first
+
+            @pl.when((side != half) & jnp.logical_not(stays))
+            def _():
+                plan_ref[0, late + jnp.where(moves, 0, 1)] = source
+
+            rank = rank + jnp.where(stays, 1, 0)
 
 
 def flat_rows(field):
@@ -160,7 +182,8 @@
     step_here = here - old
     slope_old = minmod(step_here, step_old)
     flux_old = None
-    for row in range(first, first + count + 1):
+    for step in range(count + 1):
+        row = first + step
         following = load(row + 1)
         step_next = following - here
         slope_here = minmod(step_next, step_here)
@@ -222,9 +245,74 @@
         sweep(lambda row: window[row], courant, store_middle, start - 2, span + 2 * reach + 4)
         sweep(lambda row: middle[row], courant, store_advected, start, span + 2 * reach)
         for place in range(rows):
-            low, high = plan[0, place], plan[0, rows + place]
-            same_ref[core, place] = advected[jnp.where(side == 0, low, high)]
-            cross_ref[core, place] = advected[jnp.where(side == 0, high, low)]
+            same_ref[core, place] = advected[jnp.where(side == 0, plan[0, place], plan[0, rows + place])]
+        for at in range(2):
+            cross_ref[core, at] = advected[plan[0, span + 3 * rows + at]]
+
+
+def early_kernel(turn, own_ref, swap_ref, own_a, own_b, plan_ref, out_ref, window, flow, middle, advected):
+    plan = plan_ref[...]
+    cores, stays, species, width = out_ref.shape
+    rows = stays + 1
+    span = PAIR * rows
+    band = lax.axis_index("band")
+    side = lax.axis_index("pair")
+    total = lax.axis_size("band") * span
+    base_a = jnp.where(lax.rem(band, 2) == 0, 2 * PAIR, 0)
+    pieces = width // LANES
+    apart = own_ref.shape[0] // (species + 1)
+    first_row = band * span - span
+    start = span + (1 - side) * rows
+
+    def courant(row):
+        at = first_row + row
+        return jnp.where((at >= 1) & (at <= total - 1), flow[row], 0.0)
+
+    def store_middle(row, value):
+        middle[row] = value
+
+    def store_advected(row, value):
+        advected[row - start] = value
+
+    for core in range(cores):
+        part = lax.bitwise_xor(lax.axis_index("spec"), turn * cores + core)
+        for ref, place in (
+            (own_ref, PAIR + side),
+            (swap_ref, PAIR + 1 - side),
+            (own_a, base_a + side),
+            (own_b, 2 * PAIR - base_a + side),
+        ):
+            for row in range(rows):
+                for piece in range(pieces):
+                    at = (part * pieces + piece) * rows + row
+                    lanes = slice(piece * LANES, (piece + 1) * LANES)
+                    window[place * rows + row, :, lanes] = ref[pl.ds(at, species, stride=apart), :]
+                    flow[place * rows + row, :, lanes] = ref[pl.ds(species * apart + at, 1), :]
+
+        sweep(lambda row: window[row], courant, store_middle, start - 2, rows + 4)
+        sweep(lambda row: middle[row], courant, store_advected, start, rows)
+        for at in range(stays):
+            out_ref[core, at] = advected[plan[0, span + 2 * rows + at]]
+
+
+def advect_early(turn, fields, plan, parts, rows, columns):
+    species = fields[0].shape[0] * LANES // (rows * columns) - 1
+    span = PAIR * rows
+    width = columns // parts
+    return pl.pallas_call(
+        functools.partial(early_kernel, turn),
+        out_shape=jax.ShapeDtypeStruct((CORES, rows - 1, species, width), jnp.float32),
+        in_specs=[VMEM] * 5,
+        out_specs=VMEM,
+        scratch_shapes=[
+            pltpu.VMEM((3 * span, species, width), jnp.float32),
+            pltpu.VMEM((3 * span, 1, width), jnp.float32),
+            pltpu.VMEM((3 * span, species, width), jnp.float32),
+            pltpu.VMEM((rows, species, width), jnp.float32),
+        ],
+        compiler_params=params(8),
+        cost_estimate=pl.CostEstimate(flops=4_000_000, bytes_accessed=400_000, transcendentals=0),
+    )(*fields, plan)
 
 
 def advect(turn, fields, plan, parts, rows, columns):
@@ -232,9 +320,10 @@
     span = PAIR * rows
     width = columns // parts
     chunk = jax.ShapeDtypeStruct((CORES, rows, species, width), jnp.float32)
+    crossing = jax.ShapeDtypeStruct((CORES, 2, species, width), jnp.float32)
     return pl.pallas_call(
         functools.partial(advect_kernel, turn),
-        out_shape=(chunk, chunk),
+        out_shape=(chunk, crossing),
         in_specs=[VMEM] * 7,
         out_specs=(VMEM, VMEM),
         scratch_shapes=[
@@ -263,8 +352,8 @@
 
 
 def chemistry_kernel(count, *refs):
-    chunks = refs[:count]
-    take_ref, net_ref, rate_ref, plan_ref, out_ref, cells = refs[count:]
+    chunks, early = refs[:count], refs[count : count + count // PAIR]
+    take_ref, net_ref, rate_ref, plan_ref, out_ref, cells = refs[count + count // PAIR :]
     plan = plan_ref[...]
     rows, lines, width = chunks[0].shape[1:]
     species = count * lines
@@ -272,12 +361,20 @@
     copies = lit_rows * width // LANES
     spec = lax.axis_index("spec")
     side = lax.axis_index("pair")
-    for at, chunk in enumerate(chunks):
+
+    def piece(at, place):
+        core = at // PAIR % CORES
+        if at % PAIR == 0:
+            return chunks[at][core, place]
+        code = plan[0, (PAIR + 1) * rows + place]
+        stayed = early[at // PAIR][core, jnp.clip(code, 0, rows - 2)]
+        return jnp.where(code < rows - 1, stayed, chunks[at][core, jnp.clip(code - (rows - 1), 0, 1)])
+
+    for at in range(count):
         source = lax.bitwise_xor(spec, at // PAIR) * PAIR + lax.bitwise_xor(side, at % PAIR)
         first = pl.multiple_of(source * lines, lines)
         for place in range(lit_rows):
-            cells[pl.ds(first, lines), place * width : (place + 1) * width] = chunk[at // PAIR % CORES, place]
-
+            cells[pl.ds(first, lines), place * width : (place + 1) * width] = piece(at, place)
     conc = cells[...]
     const = jnp.concatenate([rate_ref[...]] * copies, axis=1)
     for _ in range(SUBSTEPS):
@@ -286,26 +383,26 @@
         rates = const * encounter / (1.0 + jnp.abs(encounter))
         conc = conc + dot(twice(net_ref[...]), split_rows(rates))
     slot_of = [plan[0, PAIR * rows + place] for place in range(rows)]
-    for at, chunk in enumerate(chunks):
+    for at in range(count):
         source = lax.bitwise_xor(spec, at // PAIR) * PAIR + lax.bitwise_xor(side, at % PAIR)
         for place in range(lit_rows, rows):
-            out_ref[pl.ds(source * (lines * rows) + slot_of[place], lines, stride=rows), :] = chunk[at // PAIR % CORES, place]
+            out_ref[pl.ds(source * (lines * rows) + slot_of[place], lines, stride=rows), :] = piece(at, place)
     for place in range(lit_rows):
         out_ref[pl.ds(slot_of[place], species, stride=rows), :] = conc[:, place * width : (place + 1) * width]
 
 
-def chemistry(chunks, take, net, rates, plan):
+def chemistry(chunks, early, take, net, rates, plan):
     rows, lines, width = chunks[0].shape[1:]
     species = len(chunks) * lines
     flat = pl.pallas_call(
         functools.partial(chemistry_kernel, len(chunks)),
         out_shape=jax.ShapeDtypeStruct((species * rows, width), jnp.float32),
-        in_specs=[VMEM] * (len(chunks) + 4),
+        in_specs=[VMEM] * (len(chunks) + len(early) + 4),
         out_specs=VMEM,
         scratch_shapes=[pltpu.VMEM((species, rows // 2 * width), jnp.float32)],
         compiler_params=params(16),
         name="chemistry",
-    )(*chunks, take, net, rates, plan)
+    )(*chunks, *early, take, net, rates, plan)
     return flat.reshape(species, rows, width)
 
 
@@ -341,6 +438,11 @@
         pairs = [(peer, peer ^ step) for peer in range(parts * PAIR)]
         return lax.ppermute(chunk, ("spec", "pair"), pairs)
 
+    early = [None] * parts
+    for turn in reversed(range(parts // CORES)):
+        block = advect_early(turn, fields[:4], plan, parts, rows, columns)
+        early[turn * CORES] = send(block, turn * CORES * PAIR + 1)
+        early[turn * CORES + 1] = send(early[turn * CORES], PAIR)
     for turn in reversed(range(parts // CORES)):
         blocks = advect(turn, fields, plan, parts, rows, columns)
         for side in range(PAIR):
@@ -350,7 +452,7 @@
         for side in range(PAIR):
             at = turn * CORES * PAIR + side
             chunks[at + PAIR] = send(chunks[at], PAIR)
-    return chemistry(chunks, take, net, rates, plan)
+    return chemistry(chunks, early, take, net, rates, plan)
 
 
 def solution(mesh):

time: 36 us -> 36.4 us (1.011)
  the two profiles are of different devices: /device:TPU:0 before, /device:TPU:17 now
where the time goes in v4:
time: 36.4 us; the launch traced here: 36.2 us
  starting transfers between devices  20.5 us (56%)
  Pallas kernels  9.32 us (26%)
  waiting for transfers between devices  5.63 us (15%)
  local copies, waits for them, and re-layouts  0.64 us (2%)
    ppermute x11, starting transfers between devices, send(): return lax.ppermute(chunk, ('spec', 'pair'), pairs)  12.8 us
    ppermute x4, starting transfers between devices, exchange(): found.append(lax.ppermute(block, 'band', couples(bands, first)))  6.41 us
    pallas_call x1, Pallas kernels, chemistry(): pl.pallas_call(functools.partial(chemistry_kernel, len(chunks)), out_shap...  3.43 us
    ppermute x1, waiting for transfers between devices, on_device(): swap = lax.ppermute(other, 'pair', couples(PAIR, 0))  2.94 us
    pallas_call x1, Pallas kernels, mechanism_tables(): pl.pallas_call(table_kernel, out_shape=(jax.ShapeDtypeStruct((2, reaction...  2.23 us
    pallas_call x2, Pallas kernels, advect(): pl.pallas_call(functools.partial(advect_kernel, turn), out_shape=(chunk,...  1.74 us
    ppermute x4, waiting for transfers between devices, exchange(): found.append(lax.ppermute(block, 'band', couples(bands, first)))  1.57 us
    ppermute x1, starting transfers between devices, on_device(): swap = lax.ppermute(other, 'pair', couples(PAIR, 0))  1.28 us
  transfers between devices with their start and end apart: 16, of which 4 were waited for; matrix products, arithmetic and copies ran while one was open for 0% of the time, Pallas kernels for 13%

profile of v4, /device:TPU:17, one launch (start us, length us, event | category | flops | bytes accessed | tf_op | source)
XLA Modules:
  0.0 36.2 jit_solution(11128754844659129240)
XLA Ops:
  0.0 0.0 copy-start.1
  0.0 1.1 %pack.1 = (f32[528,128]{1,0:T(8,128)S(1)}, f32[528,128]{1,0:T(8,128)S(1)}) custom-call(f32[1024,128]{1,0:T(8,128)} %bitcast.17, f32[16,128]{1,0:T(8,128)} %bitcast.18), custom_call_target="tpu_custom_call" | custom-call | tf_op jit(solution)/shard_map/pack/pallas_call | solution.py:162
  1.1 0.0 copy-start
  1.1 1.3 %collective-permute-start = (f32[528,128]{1,0:T(8,128)S(1)}, f32[528,128]{1,0:T(8,128)S(1)}, u32[]{:S(2)}, u32[]{:S(2)}) collective-permute-start(f32[528,128]{1,0:T(8,128)S(1)} %get-tuple-element.16), channel_id=1, source_target_pairs={{0,1},{1,0},{2,3},{3,2},{4,5},{5,4},{6,7},{7,6},{8,9},{9,8},{10,11... | collective-permute-start | bytes 811016 | tf_op jit(solution)/shard_map/ppermute | solution.py:421
  2.4 1.3 %collective-permute-start.1 = (f32[528,128]{1,0:T(8,128)S(1)}, f32[528,128]{1,0:T(8,128)S(1)}, u32[]{:S(2)}, u32[]{:S(2)}) collective-permute-start(f32[528,128]{1,0:T(8,128)S(1)} %get-tuple-element.15.own_ref), channel_id=1, source_target_pairs={{0,2},{2,0},{4,6},{6,4},{1,3},{3,1},{5,7},{7,5},{8,10},{10,8},{12,... | collective-permute-start | bytes 811016 | tf_op jit(solution)/shard_map/ppermute | solution.py:426
  3.7 1.9 %collective-permute-start.2 = (f32[528,128]{1,0:T(8,128)S(1)}, f32[528,128]{1,0:T(8,128)S(1)}, u32[]{:S(2)}, u32[]{:S(2)}) collective-permute-start(f32[528,128]{1,0:T(8,128)S(1)} %get-tuple-element.15.own_ref), channel_id=1, source_target_pairs={{2,4},{4,2},{3,5},{5,3},{10,12},{12,10},{11,13},{13,11},{18,20},{2... | collective-permute-start | bytes 811016 | tf_op jit(solution)/shard_map/ppermute | solution.py:426
  5.6 2.9 %collective-permute-done.swap_ref = f32[528,128]{1,0:T(8,128)S(1)} collective-permute-done((f32[528,128]{1,0:T(8,128)S(1)}, f32[528,128]{1,0:T(8,128)S(1)}, u32[]{:S(2)}, u32[]{:S(2)}) %collective-permute-start) | collective-permute-done | bytes 270368 | tf_op jit(solution)/shard_map/ppermute | solution.py:421
  8.6 1.3 %collective-permute-start.3 = (f32[528,128]{1,0:T(8,128)S(1)}, f32[528,128]{1,0:T(8,128)S(1)}, u32[]{:S(2)}, u32[]{:S(2)}) collective-permute-start(f32[528,128]{1,0:T(8,128)S(1)} %collective-permute-done.swap_ref), channel_id=1, source_target_pairs={{0,2},{2,0},{4,6},{6,4},{1,3},{3,1},{5,7},{7,5},{8,10},{10,8},{12,... | collective-permute-start | bytes 811016 | tf_op jit(solution)/shard_map/ppermute | solution.py:426
  9.9 1.9 %collective-permute-start.4 = (f32[528,128]{1,0:T(8,128)S(1)}, f32[528,128]{1,0:T(8,128)S(1)}, u32[]{:S(2)}, u32[]{:S(2)}) collective-permute-start(f32[528,128]{1,0:T(8,128)S(1)} %collective-permute-done.swap_ref), channel_id=1, source_target_pairs={{2,4},{4,2},{3,5},{5,3},{10,12},{12,10},{11,13},{13,11},{18,20},{2... | collective-permute-start | bytes 811016 | tf_op jit(solution)/shard_map/ppermute | solution.py:426
  11.8 0.0 copy-start.3
  11.8 0.0 copy-start.4
  11.8 0.0 copy-done.1
  11.8 0.0 copy-done.2
  11.8 0.0 copy-done
  11.8 0.6 %copy-done.3 = s32[32]{0:T(128)S(1)} copy-done((s32[32]{0:T(128)S(1)}, s32[32]{0:T(128)}, u32[]{:S(2)}) %copy-start.3) | copy-done | bytes 152
  12.4 0.0 copy-done.4
  12.5 2.2 %tables.1 = (bf16[2,1024,256]{2,1,0:T(8,128)(2,1)S(1)}, bf16[256,1024]{1,0:T(8,128)(2,1)S(1)}, f32[1024,128]{1,0:T(8,128)S(1)}, s32[1,22]{1,0:T(1,128)S(1)}) custom-call(s32[2,1024]{1,0:T(2,128)S(1)} %bitcast.14, s32[2,1024]{1,0:T(2,128)S(1)} %bitcast.15, f32[8,128]{1,0:T(8,128)S(1)} %bitcast.16, s32[32]{0:T(128)S(1)} %copy-done.3, s32[32]{0:T(128)S(1)} %copy-done.4), custom_call_target="tpu_custom_call" | custom-call | flops 20000000 | bytes 2000000 | tf_op jit(solution)/shard_map/tables/pallas_call | solution.py:54
  14.7 0.0 collective-permute-done.1.own_a
  14.7 0.0 collective-permute-done.2.own_b
  14.7 0.4 %shard_map.75 = f32[2,3,32,128]{3,2,1,0:T(8,128)S(1)} custom-call(f32[528,128]{1,0:T(8,128)S(1)} %get-tuple-element.15.own_ref, f32[528,128]{1,0:T(8,128)S(1)} %collective-permute-done.swap_ref, f32[528,128]{1,0:T(8,128)S(1)} %collective-permute-done.1.own_a, f32[528,128]{1,0:T(8,128)S(1)} %collective-permute-done.2.own_b, ...), custom_call_target="tpu_custom_call" | custom-call | flops 4000000 | bytes 400000 | tf_op jit(solution)/shard_map/pallas_call | solution.py:302
  15.1 1.3 %collective-permute-start.12 = (f32[2,3,32,128]{3,2,1,0:T(8,128)S(1)}, f32[2,3,32,128]{3,2,1,0:T(8,128)S(1)}, u32[]{:S(2)}, u32[]{:S(2)}) collective-permute-start(f32[2,3,32,128]{3,2,1,0:T(8,128)S(1)} %shard_map.75), channel_id=1, source_target_pairs={{0,1},{1,0},{8,9},{9,8},{16,17},{17,16},{24,25},{25,24},{2,3},{3,2... | collective-permute-start | bytes 294920 | tf_op jit(solution)/shard_map/ppermute | solution.py:439
  16.4 0.0 collective-permute-done.3.swap_a
  16.4 1.6 %collective-permute-done.4.swap_b = f32[528,128]{1,0:T(8,128)S(1)} collective-permute-done((f32[528,128]{1,0:T(8,128)S(1)}, f32[528,128]{1,0:T(8,128)S(1)}, u32[]{:S(2)}, u32[]{:S(2)}) %collective-permute-start.4) | collective-permute-done | bytes 270368 | tf_op jit(solution)/shard_map/ppermute | solution.py:426
  18.0 0.9 %shard_map.74 = (f32[2,4,32,128]{3,2,1,0:T(8,128)S(1)}, f32[2,2,32,128]{3,2,1,0:T(8,128)S(1)}) custom-call(f32[528,128]{1,0:T(8,128)S(1)} %get-tuple-element.15.own_ref, f32[528,128]{1,0:T(8,128)S(1)} %collective-permute-done.swap_ref, f32[528,128]{1,0:T(8,128)S(1)} %collective-permute-done.1.own_a, f32[528,128]{1,0:T(8,128)S(1)} %collective-permute-done.2.own_b, ...), custom_call_target="tpu_custom_call" | custom-call | flops 4000000 | bytes 400000 | tf_op jit(solution)/shard_map/pallas_call | solution.py:324
  18.8 1.3 %collective-permute-start.8 = (f32[2,4,32,128]{3,2,1,0:T(8,128)S(1)}, f32[2,4,32,128]{3,2,1,0:T(8,128)S(1)}, u32[]{:S(2)}, u32[]{:S(2)}) collective-permute-start(f32[2,4,32,128]{3,2,1,0:T(8,128)S(1)} %get-tuple-element.20), channel_id=1, source_target_pairs={{0,16},{1,17},{8,24},{9,25},{16,0},{17,1},{24,8},{25,9},{2,18},{3,... | collective-permute-start | bytes 393224 | tf_op jit(solution)/shard_map/ppermute | solution.py:439
  20.2 0.4 %shard_map.76 = f32[2,3,32,128]{3,2,1,0:T(8,128)S(1)} custom-call(f32[528,128]{1,0:T(8,128)S(1)} %get-tuple-element.15.own_ref, f32[528,128]{1,0:T(8,128)S(1)} %collective-permute-done.swap_ref, f32[528,128]{1,0:T(8,128)S(1)} %collective-permute-done.1.own_a, f32[528,128]{1,0:T(8,128)S(1)} %collective-permute-done.2.own_b, ...), custom_call_target="tpu_custom_call" | custom-call | flops 4000000 | bytes 400000 | tf_op jit(solution)/shard_map/pallas_call | solution.py:302
  20.6 1.2 %collective-permute-start.14 = (f32[2,3,32,128]{3,2,1,0:T(8,128)S(1)}, f32[2,3,32,128]{3,2,1,0:T(8,128)S(1)}, u32[]{:S(2)}, u32[]{:S(2)}) collective-permute-start(f32[2,3,32,128]{3,2,1,0:T(8,128)S(1)} %shard_map.76), channel_id=1, source_target_pairs={{0,17},{1,16},{8,25},{9,24},{16,1},{17,0},{24,9},{25,8},{2,19},{3,... | collective-permute-start | bytes 294920 | tf_op jit(solution)/shard_map/ppermute | solution.py:439
  21.8 0.0 collective-permute-done.12.refs_8_
  21.8 3.2 %collective-permute-start.13 = (f32[2,3,32,128]{3,2,1,0:T(8,128)S(1)}, f32[2,3,32,128]{3,2,1,0:T(8,128)S(1)}, u32[]{:S(2)}, u32[]{:S(2)}) collective-permute-start(f32[2,3,32,128]{3,2,1,0:T(8,128)S(1)} %collective-permute-done.12.refs_8_), channel_id=1, source_target_pairs={{0,8},{1,9},{8,0},{9,1},{16,24},{17,25},{24,16},{25,17},{2,10},{3,... | collective-permute-start | bytes 294920 | tf_op jit(solution)/shard_map/ppermute | solution.py:439
  25.0 1.2 %collective-permute-start.9 = (f32[2,2,32,128]{3,2,1,0:T(8,128)S(1)}, f32[2,2,32,128]{3,2,1,0:T(8,128)S(1)}, u32[]{:S(2)}, u32[]{:S(2)}) collective-permute-start(f32[2,2,32,128]{3,2,1,0:T(8,128)S(1)} %get-tuple-element.21), channel_id=1, source_target_pairs={{0,17},{1,16},{8,25},{9,24},{16,1},{17,0},{24,9},{25,8},{2,19},{3,... | collective-permute-start | bytes 196616 | tf_op jit(solution)/shard_map/ppermute | solution.py:439
  26.2 0.9 %shard_map.73 = (f32[2,4,32,128]{3,2,1,0:T(8,128)S(1)}, f32[2,2,32,128]{3,2,1,0:T(8,128)S(1)}) custom-call(f32[528,128]{1,0:T(8,128)S(1)} %get-tuple-element.15.own_ref, f32[528,128]{1,0:T(8,128)S(1)} %collective-permute-done.swap_ref, f32[528,128]{1,0:T(8,128)S(1)} %collective-permute-done.1.own_a, f32[528,128]{1,0:T(8,128)S(1)} %collective-permute-done.2.own_b, ...), custom_call_target="tpu_custom_call" | custom-call | flops 4000000 | bytes 400000 | tf_op jit(solution)/shard_map/pallas_call | solution.py:324
  27.1 1.3 %collective-permute-start.5 = (f32[2,2,32,128]{3,2,1,0:T(8,128)S(1)}, f32[2,2,32,128]{3,2,1,0:T(8,128)S(1)}, u32[]{:S(2)}, u32[]{:S(2)}) collective-permute-start(f32[2,2,32,128]{3,2,1,0:T(8,128)S(1)} %get-tuple-element.19), channel_id=1, source_target_pairs={{0,1},{1,0},{8,9},{9,8},{16,17},{17,16},{24,25},{25,24},{2,3},{3,2... | collective-permute-start | bytes 196616 | tf_op jit(solution)/shard_map/ppermute | solution.py:439
  28.4 0.0 collective-permute-done.14.refs_10_
  28.4 0.8 %collective-permute-start.6 = (f32[2,4,32,128]{3,2,1,0:T(8,128)S(1)}, f32[2,4,32,128]{3,2,1,0:T(8,128)S(1)}, u32[]{:S(2)}, u32[]{:S(2)}) collective-permute-start(f32[2,4,32,128]{3,2,1,0:T(8,128)S(1)} %get-tuple-element.18.refs_0_), channel_id=1, source_target_pairs={{0,8},{1,9},{8,0},{9,1},{16,24},{17,25},{24,16},{25,17},{2,10},{3,... | collective-permute-start | bytes 393224 | tf_op jit(solution)/shard_map/ppermute | solution.py:439
  29.2 0.0 collective-permute-done.8.refs_4_
  29.2 0.0 collective-permute-start.10
  29.2 0.0 collective-permute-done.13.refs_9_
  29.2 0.5 %collective-permute-start.15 = (f32[2,3,32,128]{3,2,1,0:T(8,128)S(1)}, f32[2,3,32,128]{3,2,1,0:T(8,128)S(1)}, u32[]{:S(2)}, u32[]{:S(2)}) collective-permute-start(f32[2,3,32,128]{3,2,1,0:T(8,128)S(1)} %collective-permute-done.14.refs_10_), channel_id=1, source_target_pairs={{0,8},{1,9},{8,0},{9,1},{16,24},{17,25},{24,16},{25,17},{2,10},{3,... | collective-permute-start | bytes 294920 | tf_op jit(solution)/shard_map/ppermute | solution.py:439
  29.7 0.0 collective-permute-done.9.refs_5_
  29.7 1.1 %collective-permute-start.11 = (f32[2,2,32,128]{3,2,1,0:T(8,128)S(1)}, f32[2,2,32,128]{3,2,1,0:T(8,128)S(1)}, u32[]{:S(2)}, u32[]{:S(2)}) collective-permute-start(f32[2,2,32,128]{3,2,1,0:T(8,128)S(1)} %collective-permute-done.9.refs_5_), channel_id=1, source_target_pairs={{0,8},{1,9},{8,0},{9,1},{16,24},{17,25},{24,16},{25,17},{2,10},{3,... | collective-permute-start | bytes 196616 | tf_op jit(solution)/shard_map/ppermute | solution.py:439
  30.8 0.2 collective-permute-done.5.refs_1_
  31.0 0.9 %collective-permute-start.7 = (f32[2,2,32,128]{3,2,1,0:T(8,128)S(1)}, f32[2,2,32,128]{3,2,1,0:T(8,128)S(1)}, u32[]{:S(2)}, u32[]{:S(2)}) collective-permute-start(f32[2,2,32,128]{3,2,1,0:T(8,128)S(1)} %collective-permute-done.5.refs_1_), channel_id=1, source_target_pairs={{0,8},{1,9},{8,0},{9,1},{16,24},{17,25},{24,16},{25,17},{2,10},{3,... | collective-permute-start | bytes 196616 | tf_op jit(solution)/shard_map/ppermute | solution.py:439
  31.9 0.0 collective-permute-done.15.refs_11_
  31.9 0.0 collective-permute-done.11.refs_7_
  31.9 0.9 %collective-permute-done.7.refs_3_ = f32[2,2,32,128]{3,2,1,0:T(8,128)S(1)} collective-permute-done((f32[2,2,32,128]{3,2,1,0:T(8,128)S(1)}, f32[2,2,32,128]{3,2,1,0:T(8,128)S(1)}, u32[]{:S(2)}, u32[]{:S(2)}) %collective-permute-start.7) | collective-permute-done | bytes 65568 | tf_op jit(solution)/shard_map/ppermute | solution.py:439
  32.8 0.0 collective-permute-done.6.refs_2_
  32.8 0.0 collective-permute-done.10.refs_6_
  32.8 3.4 %chemistry.1 = f32[1024,128]{1,0:T(8,128)} custom-call(f32[2,4,32,128]{3,2,1,0:T(8,128)S(1)} %get-tuple-element.18.refs_0_, f32[2,2,32,128]{3,2,1,0:T(8,128)S(1)} %collective-permute-done.5.refs_1_, f32[2,4,32,128]{3,2,1,0:T(8,128)S(1)} %collective-permute-done.6.refs_2_, f32[2,2,32,128]{3,2,1,0:T(8,128)S(1)} %collective-permute-done.7.refs_3_, ...), custom_call_target="tpu_custom_call" | custom-call | tf_op jit(solution)/shard_map/chemistry/pallas_call | solution.py:397
  (1 shorter events, 0.0 us)
Async XLA Ops:
  0.0 11.8 %copy-start.1 = (s32[1024,2]{0,1:T(2,128)S(1)}, s32[1024,2]{0,1:T(2,128)}, u32[]{:S(2)}) copy-start(s32[1024,2]{0,1:T(2,128)} %param.11) | copy-start | bytes 24580
  0.0 11.8 %copy-start.2 = (f32[1024]{0:T(1024)S(1)}, f32[1024]{0:T(1024)}, u32[]{:S(2)}) copy-start(f32[1024]{0:T(1024)} %param.9) | copy-start | bytes 12292
  1.1 10.7 %copy-start = (s32[1024,2]{0,1:T(2,128)S(1)}, s32[1024,2]{0,1:T(2,128)}, u32[]{:S(2)}) copy-start(s32[1024,2]{0,1:T(2,128)} %param.10) | copy-start | bytes 24580
  1.1 7.4 %collective-permute-start = (f32[528,128]{1,0:T(8,128)S(1)}, f32[528,128]{1,0:T(8,128)S(1)}, u32[]{:S(2)}, u32[]{:S(2)}) collective-permute-start(f32[528,128]{1,0:T(8,128)S(1)} %get-tuple-element.16), channel_id=1, source_target_pairs={{0,1},{1,0},{2,3},{3,2},{4,5},{5,4},{6,7},{7,6},{8,9},{9,8},{10,11... | collective-permute-start | bytes 811016 | tf_op jit(solution)/shard_map/ppermute | solution.py:421
  2.4 12.3 %collective-permute-start.1 = (f32[528,128]{1,0:T(8,128)S(1)}, f32[528,128]{1,0:T(8,128)S(1)}, u32[]{:S(2)}, u32[]{:S(2)}) collective-permute-start(f32[528,128]{1,0:T(8,128)S(1)} %get-tuple-element.15.own_ref), channel_id=1, source_target_pairs={{0,2},{2,0},{4,6},{6,4},{1,3},{3,1},{5,7},{7,5},{8,10},{10,8},{12,... | collective-permute-start | bytes 811016 | tf_op jit(solution)/shard_map/ppermute | solution.py:426
  3.7 11.0 %collective-permute-start.2 = (f32[528,128]{1,0:T(8,128)S(1)}, f32[528,128]{1,0:T(8,128)S(1)}, u32[]{:S(2)}, u32[]{:S(2)}) collective-permute-start(f32[528,128]{1,0:T(8,128)S(1)} %get-tuple-element.15.own_ref), channel_id=1, source_target_pairs={{2,4},{4,2},{3,5},{5,3},{10,12},{12,10},{11,13},{13,11},{18,20},{2... | collective-permute-start | bytes 811016 | tf_op jit(solution)/shard_map/ppermute | solution.py:426
  8.6 7.8 %collective-permute-start.3 = (f32[528,128]{1,0:T(8,128)S(1)}, f32[528,128]{1,0:T(8,128)S(1)}, u32[]{:S(2)}, u32[]{:S(2)}) collective-permute-start(f32[528,128]{1,0:T(8,128)S(1)} %collective-permute-done.swap_ref), channel_id=1, source_target_pairs={{0,2},{2,0},{4,6},{6,4},{1,3},{3,1},{5,7},{7,5},{8,10},{10,8},{12,... | collective-permute-start | bytes 811016 | tf_op jit(solution)/shard_map/ppermute | solution.py:426
  9.9 8.1 %collective-permute-start.4 = (f32[528,128]{1,0:T(8,128)S(1)}, f32[528,128]{1,0:T(8,128)S(1)}, u32[]{:S(2)}, u32[]{:S(2)}) collective-permute-start(f32[528,128]{1,0:T(8,128)S(1)} %collective-permute-done.swap_ref), channel_id=1, source_target_pairs={{2,4},{4,2},{3,5},{5,3},{10,12},{12,10},{11,13},{13,11},{18,20},{2... | collective-permute-start | bytes 811016 | tf_op jit(solution)/shard_map/ppermute | solution.py:426
  11.8 0.7 %copy-start.3 = (s32[32]{0:T(128)S(1)}, s32[32]{0:T(128)}, u32[]{:S(2)}) copy-start(s32[32]{0:T(128)} %slot_ref.1) | copy-start | bytes 388
  11.8 0.7 %copy-start.4 = (s32[32]{0:T(128)S(1)}, s32[32]{0:T(128)}, u32[]{:S(2)}) copy-start(s32[32]{0:T(128)} %day_ref.1) | copy-start | bytes 388
  15.1 6.7 %collective-permute-start.12 = (f32[2,3,32,128]{3,2,1,0:T(8,128)S(1)}, f32[2,3,32,128]{3,2,1,0:T(8,128)S(1)}, u32[]{:S(2)}, u32[]{:S(2)}) collective-permute-start(f32[2,3,32,128]{3,2,1,0:T(8,128)S(1)} %shard_map.75), channel_id=1, source_target_pairs={{0,1},{1,0},{8,9},{9,8},{16,17},{17,16},{24,25},{25,24},{2,3},{3,2... | collective-permute-start | bytes 294920 | tf_op jit(solution)/shard_map/ppermute | solution.py:439
  18.8 10.3 %collective-permute-start.8 = (f32[2,4,32,128]{3,2,1,0:T(8,128)S(1)}, f32[2,4,32,128]{3,2,1,0:T(8,128)S(1)}, u32[]{:S(2)}, u32[]{:S(2)}) collective-permute-start(f32[2,4,32,128]{3,2,1,0:T(8,128)S(1)} %get-tuple-element.20), channel_id=1, source_target_pairs={{0,16},{1,17},{8,24},{9,25},{16,0},{17,1},{24,8},{25,9},{2,18},{3,... | collective-permute-start | bytes 393224 | tf_op jit(solution)/shard_map/ppermute | solution.py:439
  20.6 7.8 %collective-permute-start.14 = (f32[2,3,32,128]{3,2,1,0:T(8,128)S(1)}, f32[2,3,32,128]{3,2,1,0:T(8,128)S(1)}, u32[]{:S(2)}, u32[]{:S(2)}) collective-permute-start(f32[2,3,32,128]{3,2,1,0:T(8,128)S(1)} %shard_map.76), channel_id=1, source_target_pairs={{0,17},{1,16},{8,25},{9,24},{16,1},{17,0},{24,9},{25,8},{2,19},{3,... | collective-permute-start | bytes 294920 | tf_op jit(solution)/shard_map/ppermute | solution.py:439
  21.8 7.4 %collective-permute-start.13 = (f32[2,3,32,128]{3,2,1,0:T(8,128)S(1)}, f32[2,3,32,128]{3,2,1,0:T(8,128)S(1)}, u32[]{:S(2)}, u32[]{:S(2)}) collective-permute-start(f32[2,3,32,128]{3,2,1,0:T(8,128)S(1)} %collective-permute-done.12.refs_8_), channel_id=1, source_target_pairs={{0,8},{1,9},{8,0},{9,1},{16,24},{17,25},{24,16},{25,17},{2,10},{3,... | collective-permute-start | bytes 294920 | tf_op jit(solution)/shard_map/ppermute | solution.py:439
  25.0 4.7 %collective-permute-start.9 = (f32[2,2,32,128]{3,2,1,0:T(8,128)S(1)}, f32[2,2,32,128]{3,2,1,0:T(8,128)S(1)}, u32[]{:S(2)}, u32[]{:S(2)}) collective-permute-start(f32[2,2,32,128]{3,2,1,0:T(8,128)S(1)} %get-tuple-element.21), channel_id=1, source_target_pairs={{0,17},{1,16},{8,25},{9,24},{16,1},{17,0},{24,9},{25,8},{2,19},{3,... | collective-permute-start | bytes 196616 | tf_op jit(solution)/shard_map/ppermute | solution.py:439
  27.1 3.9 %collective-permute-start.5 = (f32[2,2,32,128]{3,2,1,0:T(8,128)S(1)}, f32[2,2,32,128]{3,2,1,0:T(8,128)S(1)}, u32[]{:S(2)}, u32[]{:S(2)}) collective-permute-start(f32[2,2,32,128]{3,2,1,0:T(8,128)S(1)} %get-tuple-element.19), channel_id=1, source_target_pairs={{0,1},{1,0},{8,9},{9,8},{16,17},{17,16},{24,25},{25,24},{2,3},{3,2... | collective-permute-start | bytes 196616 | tf_op jit(solution)/shard_map/ppermute | solution.py:439
  28.4 4.4 %collective-permute-start.6 = (f32[2,4,32,128]{3,2,1,0:T(8,128)S(1)}, f32[2,4,32,128]{3,2,1,0:T(8,128)S(1)}, u32[]{:S(2)}, u32[]{:S(2)}) collective-permute-start(f32[2,4,32,128]{3,2,1,0:T(8,128)S(1)} %get-tuple-element.18.refs_0_), channel_id=1, source_target_pairs={{0,8},{1,9},{8,0},{9,1},{16,24},{17,25},{24,16},{25,17},{2,10},{3,... | collective-permute-start | bytes 393224 | tf_op jit(solution)/shard_map/ppermute | solution.py:439
  29.2 3.6 %collective-permute-start.10 = (f32[2,4,32,128]{3,2,1,0:T(8,128)S(1)}, f32[2,4,32,128]{3,2,1,0:T(8,128)S(1)}, u32[]{:S(2)}, u32[]{:S(2)}) collective-permute-start(f32[2,4,32,128]{3,2,1,0:T(8,128)S(1)} %collective-permute-done.8.refs_4_), channel_id=1, source_target_pairs={{0,8},{1,9},{8,0},{9,1},{16,24},{17,25},{24,16},{25,17},{2,10},{3,... | collective-permute-start | bytes 393224 | tf_op jit(solution)/shard_map/ppermute | solution.py:439
  29.2 2.7 %collective-permute-start.15 = (f32[2,3,32,128]{3,2,1,0:T(8,128)S(1)}, f32[2,3,32,128]{3,2,1,0:T(8,128)S(1)}, u32[]{:S(2)}, u32[]{:S(2)}) collective-permute-start(f32[2,3,32,128]{3,2,1,0:T(8,128)S(1)} %collective-permute-done.14.refs_10_), channel_id=1, source_target_pairs={{0,8},{1,9},{8,0},{9,1},{16,24},{17,25},{24,16},{25,17},{2,10},{3,... | collective-permute-start | bytes 294920 | tf_op jit(solution)/shard_map/ppermute | solution.py:439
  29.7 2.2 %collective-permute-start.11 = (f32[2,2,32,128]{3,2,1,0:T(8,128)S(1)}, f32[2,2,32,128]{3,2,1,0:T(8,128)S(1)}, u32[]{:S(2)}, u32[]{:S(2)}) collective-permute-start(f32[2,2,32,128]{3,2,1,0:T(8,128)S(1)} %collective-permute-done.9.refs_5_), channel_id=1, source_target_pairs={{0,8},{1,9},{8,0},{9,1},{16,24},{17,25},{24,16},{25,17},{2,10},{3,... | collective-permute-start | bytes 196616 | tf_op jit(solution)/shard_map/ppermute | solution.py:439
  31.0 1.8 %collective-permute-start.7 = (f32[2,2,32,128]{3,2,1,0:T(8,128)S(1)}, f32[2,2,32,128]{3,2,1,0:T(8,128)S(1)}, u32[]{:S(2)}, u32[]{:S(2)}) collective-permute-start(f32[2,2,32,128]{3,2,1,0:T(8,128)S(1)} %collective-permute-done.5.refs_1_), channel_id=1, source_target_pairs={{0,8},{1,9},{8,0},{9,1},{16,24},{17,25},{24,16},{25,17},{2,10},{3,... | collective-permute-start | bytes 196616 | tf_op jit(solution)/shard_map/ppermute | solution.py:439
